TPU v7x, 512 devices: a whole 4x4x16 slice. The times are simulated.
512 devices in a mesh: dom: 512 (over z, y, x, core).
Axes of the slice: x: 4, y: 4, z: 16, core: 2. Of those that a mesh axis runs over, the one named last changes fastest.
Arguments:
- particles: float32 [512, 2, 256, 128], P('dom'), may hold values from -60 to 60
- offspring: int32 [512], P('dom'), may hold values from 0 to 7, as said below
- noise: float32 [2, 512, 2, 256, 128], P(None, 'dom'), may hold values from -6 to 6
- accept: int32 [2, 512], P(None, 'dom'), may hold values 0 or 1
- observed: float32 [256, 256], replicated, may hold values from -6 to 6
Outputs:
- moved: float32 [512, 2, 256, 128], P('dom')
- misfit: float32 [2, 512], P(None, 'dom')
Inputs may be any that keep to these rules, and one draw needn't show every extreme that they name: `offspring`: the counts sum to 512. Slot s, numbered by the counts' running sum, is filled by a particle at most 3 places from s, and in every draw some slot is filled from exactly 3 places away.
All inputs are finite; a program needn't handle non-finite values. No bound on the sum of `accept` on one device may be relied on, other than what follows from the above.
Results may differ from a plain program's by a relative error of at most 0.0001.
Values sent between devices are 32-bit elements; how exact they have to be, the bound alone decides.
No kernel may reach another device: no remote copies, remote signals or barrier semaphores. Data moves between devices by JAX's collectives and lax.ppermute only.
A program may use at most 64 MiB of HBM per device.

v0:
```python
import math

import jax
import jax.numpy as jnp
from jax import lax
from jax.sharding import PartitionSpec as P

MOVES = 2
SPAN = 3
LOW = 16


time_step = 0.05
viscosity = 0.001
noise_level = 0.5
spectral_scale = 64.0
prior_amplitude = 1.5
step_size = 0.4
highest = lax.Precision.HIGHEST


def carried_in(part, axis, combine, identity):
    place = lax.axis_index(axis)
    gathered = lax.all_gather(part, axis)
    state = jnp.zeros_like(part) + jnp.asarray(identity, part.dtype)

    def one(lap, state):
        return combine(state, lax.dynamic_index_in_dim(gathered, lap, 0, False))

    return lax.fori_loop(0, place, one, state)


def from_behind(value, axis, steps):
    count = lax.axis_size(axis)
    leading, last = (max(0, -steps), min(count, count - steps))
    return lax.ppermute(value, axis, [(source, source + steps) for source in range(leading, last)])


def tables(grid):
    half = grid // 2
    index_a = jnp.arange(grid)
    phase_y = (index_a[:, None] * index_a[None, :] % grid).astype(jnp.float32) * (
        2.0 * math.pi / grid
    )
    cos_y = jnp.cos(phase_y)
    sin_y = jnp.sin(phase_y)
    index_q = jnp.arange(half)
    phase_x = (index_q[:, None] * index_a[None, :] % grid).astype(jnp.float32) * (
        2.0 * math.pi / grid
    )
    weight = jnp.where(index_q == 0, 1.0, 2.0).astype(jnp.float32)[:, None]
    backward_table = (
        jnp.concatenate([weight * jnp.cos(phase_x), -weight * jnp.sin(phase_x)], axis=0)
        / spectral_scale
    )
    fore_table = jnp.concatenate([jnp.cos(phase_x).T, -jnp.sin(phase_x).T], axis=1) * (
        spectral_scale / (grid * grid)
    )
    return (cos_y, sin_y, backward_table, fore_table)


def synthesize(real_part, imag_part, lookup_tables):
    cos_y, sin_y, backward_table, fore_table = lookup_tables
    half = real_part.shape[-1]
    stacked = jnp.concatenate([real_part, imag_part], axis=-1)
    with_cos = jnp.einsum("ap,bpq->baq", cos_y, stacked, precision=highest)
    with_sin = jnp.einsum("ap,bpq->baq", sin_y, stacked, precision=highest)
    rows_re = with_cos[..., :half] - with_sin[..., half:]
    rows_im = with_sin[..., :half] + with_cos[..., half:]
    joined = jnp.concatenate([rows_re, rows_im], axis=-1)
    return jnp.einsum("baq,qc->bac", joined, backward_table, precision=highest)


def analyse(field, lookup_tables):
    cos_y, sin_y, backward_table, fore_table = lookup_tables
    half = field.shape[-1] // 2
    rows = jnp.einsum("bac,cq->baq", field, fore_table, precision=highest)
    with_cos = jnp.einsum("ap,baq->bpq", cos_y, rows, precision=highest)
    with_sin = jnp.einsum("ap,baq->bpq", sin_y, rows, precision=highest)
    return (
        with_cos[..., :half] + with_sin[..., half:],
        with_cos[..., half:] - with_sin[..., :half],
    )


def wavenumbers(grid):
    index_y = jnp.arange(grid)
    wave_y = jnp.where(index_y < grid // 2, index_y, index_y - grid).astype(jnp.float32)[:, None]
    wave_x = jnp.arange(grid // 2).astype(jnp.float32)[None, :]
    return (wave_y, wave_x)


def predicted_state(present_state, observed, lookup_tables):
    grid = present_state.shape[2]
    count = present_state.shape[0]
    wave_y, wave_x = wavenumbers(grid)
    wave_sq = wave_y * wave_y + wave_x * wave_x
    inverse_sq = jnp.where(wave_sq > 0, 1.0 / jnp.maximum(wave_sq, 1.0), 0.0)
    keeper = ((jnp.abs(wave_y) <= grid // 3) & (wave_x <= grid // 3)).astype(jnp.float32)
    damping = 1.0 + time_step * viscosity * wave_sq
    real_part = present_state[:, 0]
    imag_part = present_state[:, 1]
    psi_re = real_part * inverse_sq
    psi_im = imag_part * inverse_sq
    fields = synthesize(
        jnp.concatenate([real_part, -wave_y * psi_im, wave_x * psi_im], axis=0),
        jnp.concatenate([imag_part, wave_y * psi_re, -wave_x * psi_re], axis=0),
        lookup_tables,
    )
    vort = fields[:count]
    products = jnp.concatenate(
        [fields[count : 2 * count] * vort, fields[2 * count :] * vort], axis=0
    )
    flux_re, flux_im = analyse(products, lookup_tables)
    nonlin_re = -(wave_x * flux_im[:count] + wave_y * flux_im[count:]) * keeper
    nonlin_im = (wave_x * flux_re[:count] + wave_y * flux_re[count:]) * keeper
    real_part = (real_part - time_step * nonlin_re) / damping
    imag_part = (imag_part - time_step * nonlin_im) / damping
    final = synthesize(real_part, imag_part, lookup_tables)
    return jnp.sum((final - observed[None]) ** 2, axis=(1, 2)) / (
        2.0 * noise_level * noise_level * grid * grid
    )


def low_modes(block):
    grid = block.shape[-2]
    return jnp.concatenate(
        [block[..., : LOW // 2, :LOW], block[..., grid - LOW // 2 :, :LOW]], axis=-2
    )


def add_counts(earlier, later):
    return earlier + later


def body(particles, offspring, noise, accept, observed):
    per_device = particles.shape[0]
    grid = particles.shape[2]
    devices = lax.axis_size("dom")
    position = lax.axis_index("dom")
    before = carried_in(jnp.sum(offspring), "dom", add_counts, jnp.int32(0))
    finish = before + jnp.cumsum(offspring)
    starts = finish - offspring
    package = (particles, starts.astype(jnp.float32), finish.astype(jnp.float32))
    gathered_values = [package]
    for distance in range(1, SPAN + 1):
        for direction in (1, -1):
            gathered_values.append(
                from_behind((package[0], package[1], package[2]), "dom", direction * distance)
            )
    candidates = jnp.concatenate([item[0] for item in gathered_values], axis=0)
    cand_start = jnp.concatenate([item[1] for item in gathered_values], axis=0)
    cand_end = jnp.concatenate([item[2] for item in gathered_values], axis=0)
    slot_ids = (position * per_device + jnp.arange(per_device, dtype=jnp.int32)).astype(jnp.float32)
    chosen = (
        (cand_start[None, :] <= slot_ids[:, None]) & (slot_ids[:, None] < cand_end[None, :])
    ).astype(jnp.float32)
    present_state = jnp.einsum("sc,cxyz->sxyz", chosen, candidates, precision=highest)
    totals = lax.psum(jnp.sum(low_modes(present_state) ** 2, axis=0), "dom")
    adapted = jnp.sqrt(totals / (per_device * devices) + 1e-06)
    wave_y, wave_x = wavenumbers(grid)
    prior = prior_amplitude / (1.0 + jnp.sqrt(wave_y * wave_y + wave_x * wave_x) / 8.0)
    spread = jnp.stack([prior, prior])
    spread = spread.at[:, : LOW // 2, :LOW].set(adapted[:, : LOW // 2])
    spread = spread.at[:, grid - LOW // 2 :, :LOW].set(adapted[:, LOW // 2 :])
    lookup_tables = tables(grid)
    keep = math.sqrt(1.0 - step_size * step_size)
    score_values = []
    for move in range(MOVES):
        candidate_state = keep * present_state + step_size * spread[None] * noise[move]
        score_values.append(predicted_state(candidate_state, observed, lookup_tables))
        present_state = jnp.where(
            accept[move][:, None, None, None] == 1, candidate_state, present_state
        )
    return (present_state, jnp.stack(score_values))


def solution(mesh):
    return jax.shard_map(
        body,
        mesh=mesh,
        in_specs=(
            P("dom", None, None, None),
            P("dom"),
            P(None, "dom", None, None, None),
            P(None, "dom"),
            P(),
        ),
        out_specs=(P("dom", None, None, None), P(None, "dom")),
        check_vma=False,
    )
```

profile of v0, /device:TPU:1, one launch (start us, length us, event | category | flops | bytes accessed | tf_op | source)
XLA Modules:
  0.0 980.4 jit_solution(8580837013161240498)
XLA Ops:
  1.4 111.0 %all-reduce = s32[512]{0:T(512)S(1)} all-reduce(s32[512]{0:T(512)S(1)} %dynamic-update-slice.8), channel_id=1, replica_groups=mesh['dom'=512] {'dom'}, use_global_device_ids=true, to_apply=%add | all-reduce | flops 512 | bytes 4096
  112.4 1.2 while.12
  112.4 0.6 dynamic_slice.5
  113.7 8.1 collective-permute-start.10
  121.8 1.3 collective-permute-start.11
  123.1 3.1 collective-permute-start.12
  126.2 1.9 collective-permute-start.13
  128.2 7.6 collective-permute-start.14
  135.8 1.0 constant_dynamic-update-slice_fusion.6
  136.9 0.5 sine_negate_fusion
  137.4 0.1 fusion.67
  137.6 1.1 fusion.185
  138.6 0.6 fusion.186
  139.2 0.5 sine_multiply_fusion
  139.8 0.1 copy.23
  139.9 0.1 copy.24
  141.4 3.9 collective-permute-start.6
  145.3 2.7 collective-permute-start.7
  148.1 6.3 collective-permute-start.8
  154.3 1.3 collective-permute-start.9
  155.6 7.6 collective-permute-start
  163.2 2.8 collective-permute-start.1
  166.0 3.8 concatenate.77
  169.9 7.6 collective-permute-start.2
  177.4 1.3 collective-permute-start.3
  178.7 11.9 %collective-permute-start.4 = (f32[1]{0:T(128)}, f32[1]{0:T(128)}, u32[]{:S(2)}, u32[]{:S(2)}) collective-permute-start(f32[1]{0:T(128)} %convert_element_type.174), channel_id=1, source_target_pairs={{0,3},{1,4},{2,5},{3,6},{4,7},{5,8},{6,9},{7,10},{8,11},{9,12},{10... | collective-permute-start | bytes 20 | tf_op jit(solution)/shard_map/ppermute | solution.py:36
  190.6 1.3 collective-permute-start.5
  191.9 1.3 collective-permute-start.15
  193.2 4.5 collective-permute-done.5
  197.7 9.1 collective-permute-start.16
  206.8 3.7 concatenate.76
  210.5 1.3 collective-permute-start.17
  211.8 1.0 constant_dynamic-update-slice_fusion.5
  212.7 1.0 constant_dynamic-update-slice_fusion.4
  213.7 1.0 constant_dynamic-update-slice_fusion.3
  214.7 1.0 constant_dynamic-update-slice_fusion.1
  215.7 5.3 collective-permute-done.17
  221.0 2.1 fusion
  223.1 0.1 copy.18
  223.4 725.5 %psum.7 = f32[2,16,16]{1,2,0:T(8,128)S(1)} all-reduce(f32[2,16,16]{1,2,0:T(8,128)S(1)} %maximum_multiply_fusion.6), channel_id=1, replica_groups=mesh['dom'=512] {'dom'}, use_global_device_ids=true, to_apply=%region_2.3 | all-reduce | flops 512 | bytes 4096 | tf_op jit(solution)/shard_map/psum | solution.py:159
  948.9 0.7 scatter.6
  949.6 1.3 scatter.9
  951.1 0.2 broadcast_multiply_fusion.4
  951.2 1.8 convolution_bitcast_fusion.1
  953.0 1.8 convolution_bitcast_fusion
  954.9 1.4 fusion.8
  956.4 0.7 fusion.18
  957.1 1.6 convolution_bitcast_fusion.4
  958.6 1.6 convolution_bitcast_fusion.5
  960.2 1.8 convolution_bitcast_fusion.3
  962.0 2.0 convolution_bitcast_fusion.2
  964.1 1.4 fusion.4
  965.5 0.7 fusion.14
  966.2 1.6 convolution_bitcast_fusion.6
  967.8 1.6 convolution_bitcast_fusion.7
  969.5 0.2 fusion.55
  969.7 1.4 convolution_bitcast_fusion.11
  971.1 1.4 convolution_bitcast_fusion.10
  972.5 1.4 convolution_bitcast_fusion.9
  973.8 1.4 convolution_bitcast_fusion.8
  975.2 1.2 fusion.12
  977.2 1.2 fusion.13
  979.0 0.8 copy.15
  979.9 0.6 pad_maximum_fusion
  (49 shorter events, 1.2 us)
Async XLA Ops:
  0.6 138.0 %copy-start.1 = (s32[2,1]{0,1:T(1,128)S(1)}, s32[2,1]{0,1:T(1,128)}, u32[]{:S(2)}) copy-start(s32[2,1]{0,1:T(1,128)} %param.14) | copy-start | bytes 28
  113.7 27.7 %collective-permute-start.10 = (f32[1]{0:T(128)}, f32[1]{0:T(128)}, u32[]{:S(2)}, u32[]{:S(2)}) collective-permute-start(f32[1]{0:T(128)} %convert_element_type.176), channel_id=1, source_target_pairs={{0,3},{1,4},{2,5},{3,6},{4,7},{5,8},{6,9},{7,10},{8,11},{9,12},{10... | collective-permute-start | bytes 20 | tf_op jit(solution)/shard_map/ppermute | solution.py:36
  121.8 23.5 %collective-permute-start.11 = (f32[1]{0:T(128)}, f32[1]{0:T(128)}, u32[]{:S(2)}, u32[]{:S(2)}) collective-permute-start(f32[1]{0:T(128)} %convert_element_type.176), channel_id=1, source_target_pairs={{3,0},{4,1},{5,2},{6,3},{7,4},{8,5},{9,6},{10,7},{11,8},{12,9},{13... | collective-permute-start | bytes 20 | tf_op jit(solution)/shard_map/ppermute | solution.py:36
  123.1 87.4 %collective-permute-start.12 = (f32[1,2,256,128]{3,2,1,0:T(8,128)}, f32[1,2,256,128]{3,2,1,0:T(8,128)}, u32[]{:S(2)}, u32[]{:S(2)}) collective-permute-start(f32[1,2,256,128]{3,2,1,0:T(8,128)} %param.11), channel_id=1, source_target_pairs={{0,1},{1,2},{2,3},{3,4},{4,5},{5,6},{6,7},{7,8},{8,9},{9,10},{10,1... | collective-permute-start | bytes 786440 | tf_op jit(solution)/shard_map/ppermute | solution.py:36
  126.2 86.5 %collective-permute-start.13 = (f32[1,2,256,128]{3,2,1,0:T(8,128)}, f32[1,2,256,128]{3,2,1,0:T(8,128)}, u32[]{:S(2)}, u32[]{:S(2)}) collective-permute-start(f32[1,2,256,128]{3,2,1,0:T(8,128)} %param.11), channel_id=1, source_target_pairs={{1,0},{2,1},{3,2},{4,3},{5,4},{6,5},{7,6},{8,7},{9,8},{10,9},{11,1... | collective-permute-start | bytes 786440 | tf_op jit(solution)/shard_map/ppermute | solution.py:36
  128.2 85.5 %collective-permute-start.14 = (f32[1,2,256,128]{3,2,1,0:T(8,128)}, f32[1,2,256,128]{3,2,1,0:T(8,128)}, u32[]{:S(2)}, u32[]{:S(2)}) collective-permute-start(f32[1,2,256,128]{3,2,1,0:T(8,128)} %param.11), channel_id=1, source_target_pairs={{0,2},{1,3},{2,4},{3,5},{4,6},{5,7},{6,8},{7,9},{8,10},{9,11},{10,... | collective-permute-start | bytes 786440 | tf_op jit(solution)/shard_map/ppermute | solution.py:36
  141.4 6.7 collective-permute-start.6
  145.3 9.0 collective-permute-start.7
  148.1 7.6 collective-permute-start.8
  154.3 8.9 collective-permute-start.9
  155.6 14.2 %collective-permute-start = (f32[1]{0:T(128)}, f32[1]{0:T(128)}, u32[]{:S(2)}, u32[]{:S(2)}) collective-permute-start(f32[1]{0:T(128)} %convert_element_type.174), channel_id=1, source_target_pairs={{0,1},{1,2},{2,3},{3,4},{4,5},{5,6},{6,7},{7,8},{8,9},{9,10},{10,1... | collective-permute-start | bytes 20 | tf_op jit(solution)/shard_map/ppermute | solution.py:36
  163.2 14.3 %collective-permute-start.1 = (f32[1]{0:T(128)}, f32[1]{0:T(128)}, u32[]{:S(2)}, u32[]{:S(2)}) collective-permute-start(f32[1]{0:T(128)} %convert_element_type.174), channel_id=1, source_target_pairs={{1,0},{2,1},{3,2},{4,3},{5,4},{6,5},{7,6},{8,7},{9,8},{10,9},{11,1... | collective-permute-start | bytes 20 | tf_op jit(solution)/shard_map/ppermute | solution.py:36
  169.9 8.9 collective-permute-start.2
  177.4 13.2 %collective-permute-start.3 = (f32[1]{0:T(128)}, f32[1]{0:T(128)}, u32[]{:S(2)}, u32[]{:S(2)}) collective-permute-start(f32[1]{0:T(128)} %convert_element_type.174), channel_id=1, source_target_pairs={{2,0},{3,1},{4,2},{5,3},{6,4},{7,5},{8,6},{9,7},{10,8},{11,9},{12,... | collective-permute-start | bytes 20 | tf_op jit(solution)/shard_map/ppermute | solution.py:36
  178.7 13.2 %collective-permute-start.4 = (f32[1]{0:T(128)}, f32[1]{0:T(128)}, u32[]{:S(2)}, u32[]{:S(2)}) collective-permute-start(f32[1]{0:T(128)} %convert_element_type.174), channel_id=1, source_target_pairs={{0,3},{1,4},{2,5},{3,6},{4,7},{5,8},{6,9},{7,10},{8,11},{9,12},{10... | collective-permute-start | bytes 20 | tf_op jit(solution)/shard_map/ppermute | solution.py:36
  190.6 7.1 collective-permute-start.5
  191.9 22.8 %collective-permute-start.15 = (f32[1,2,256,128]{3,2,1,0:T(8,128)}, f32[1,2,256,128]{3,2,1,0:T(8,128)S(1)}, u32[]{:S(2)}, u32[]{:S(2)}) collective-permute-start(f32[1,2,256,128]{3,2,1,0:T(8,128)} %param.11), channel_id=1, source_target_pairs={{2,0},{3,1},{4,2},{5,3},{6,4},{7,5},{8,6},{9,7},{10,8},{11,9},{12,... | collective-permute-start | bytes 786440 | tf_op jit(solution)/shard_map/ppermute | solution.py:36
  197.7 17.0 %collective-permute-start.16 = (f32[1,2,256,128]{3,2,1,0:T(8,128)}, f32[1,2,256,128]{3,2,1,0:T(8,128)}, u32[]{:S(2)}, u32[]{:S(2)}) collective-permute-start(f32[1,2,256,128]{3,2,1,0:T(8,128)} %param.11), channel_id=1, source_target_pairs={{0,3},{1,4},{2,5},{3,6},{4,7},{5,8},{6,9},{7,10},{8,11},{9,12},{10... | collective-permute-start | bytes 786440 | tf_op jit(solution)/shard_map/ppermute | solution.py:36
  210.5 10.6 %collective-permute-start.17 = (f32[1,2,256,128]{3,2,1,0:T(8,128)}, f32[1,2,256,128]{3,2,1,0:T(8,128)S(1)}, u32[]{:S(2)}, u32[]{:S(2)}) collective-permute-start(f32[1,2,256,128]{3,2,1,0:T(8,128)} %param.11), channel_id=1, source_target_pairs={{3,0},{4,1},{5,2},{6,3},{7,4},{8,5},{9,6},{10,7},{11,8},{12,9},{13... | collective-permute-start | bytes 786440 | tf_op jit(solution)/shard_map/ppermute | solution.py:36
  972.5 2.8 copy-start
where the time goes:
time: 999 us; the launch traced here: 980 us
  blocking collectives  836 us (84%)
  starting transfers between devices  80.4 us (8%)
  matrix products  27.6 us (3%)
  local copies, waits for them, and re-layouts  18.2 us (2%)
    psum x1, blocking collectives, body(): totals = lax.psum(jnp.sum(low_modes(present_state) ** 2, axis=0), 'dom')  725 us
    unnamed x1, blocking collectives  111 us
    ppermute x18, starting transfers between devices, from_behind(): lax.ppermute(value, axis, [(source, source + steps) for source in range(l...  80.4 us
  transfers between devices with their start and end apart: 18, of which 2 were waited for; matrix products, arithmetic and copies ran while one was open for 2% of the time, Pallas kernels for 0%

commit v1 on v0

v1 whole, which is shorter than its diff:
```python
import functools
import math

import jax
import jax.numpy as jnp
import numpy as np
from jax import lax
from jax.experimental import pallas as pl
from jax.experimental.pallas import tpu as pltpu
from jax.sharding import PartitionSpec as P

MOVES = 2
LOW = 16
GRID = 256
HALF = 128
CUT = GRID // 3
BAND = 96
RING = 16
PLANE = 32
COUNTS = 64

time_step = 0.05
viscosity = 0.001
noise_level = 0.5
prior_amplitude = 1.5
step_size = 0.4
keep = math.sqrt(1.0 - step_size * step_size)

f32 = jnp.float32
bf16 = jnp.bfloat16


def split_table(table):
    high = table.astype(bf16)
    low = (table - high.astype(np.float64)).astype(bf16)
    return high, low


@functools.lru_cache(maxsize=1)
def tables():
    index = np.arange(GRID)
    phase = (index[:, None] * index[None, :] % GRID) * (2.0 * np.pi / GRID)
    cos, sin = np.cos(phase), np.sin(phase)
    across = np.concatenate([cos, sin], axis=1)
    down = np.concatenate([cos[:HALF], sin[:HALF]], axis=0)
    back = np.concatenate([cos[:, :HALF], sin[:, :HALF]], axis=1)
    parts = split_table(across) + split_table(down) + split_table(back)
    return np.concatenate(parts, axis=1)


def lanes(shape):
    return lax.broadcasted_iota(jnp.int32, shape, len(shape) - 1)


def first_kernel(ring_at, offspring_ref, top_ref, bottom_ref, tile_ref):
    count = offspring_ref[0].astype(f32)
    lane = lanes((8, 128))
    tile = jnp.where(lane == COUNTS + ring_at(), count, 0.0)
    for part in range(2):
        for side, ref in enumerate((top_ref, bottom_ref)):
            low = jnp.where(lane < LOW, ref[0, part], 0.0)
            square = count * (low * low)
            shift = (2 * part + side) * LOW
            tile += pltpu.roll(square, shift, 1) if shift else square
    tile_ref[...] = jnp.broadcast_to(tile[None], tile_ref.shape)


def second_kernel(tiles_ref, tile_ref):
    total = tiles_ref[0]
    for at in range(1, RING):
        total += tiles_ref[at]
    tile_ref[...] = jnp.broadcast_to(total[None], tile_ref.shape)


def split(value):
    high = value.astype(bf16)
    return high, (value - high.astype(f32)).astype(bf16)


def product(left_high, left_low, right_high, right_low):
    dot = functools.partial(jnp.dot, preferred_element_type=f32)
    return (
        dot(left_high, right_high) + dot(left_low, right_high) + dot(left_high, right_low)
    )


def final_kernel(
    slot_at,
    accept_ref,
    tiles_ref,
    own_ref,
    behind_ref,
    ahead_ref,
    partner_ref,
    far_ref,
    partner_behind_ref,
    partner_ahead_ref,
    noise_ref,
    observed_ref,
    table_ref,
    moved_ref,
    misfit_ref,
    chosen,
    moved_buf,
    data_high,
    data_low,
    in_sem,
    out_sem,
):
    across_high, across_low, down_high, down_low, back_high, back_low = (
        table_ref.at[:, start : start + size]
        for start, size in ((0, 512), (512, 512), (1024, 256), (1280, 256), (1536, 256), (1792, 256))
    )
    slot = slot_at()
    odd = lax.rem(slot, 2)

    counts = tiles_ref[:, 0, :]
    lane = lanes((PLANE, 128))
    plane_at = lax.broadcasted_iota(jnp.int32, (PLANE, 128), 0)
    place = (lane - COUNTS) * PLANE + plane_at
    counted = (lane >= COUNTS) & (lane < COUNTS + RING)
    offset = jnp.full((1, 1), -3, jnp.int32)
    for distance in range(-3, 4):
        ends = jnp.sum(
            jnp.where(counted & (place <= slot + distance), counts, 0.0), keepdims=True
        )
        offset += (ends <= slot.astype(f32)).astype(jnp.int32)
    offset = jnp.minimum(offset, 3)[0, 0]

    side = 1 - 2 * odd
    candidates = (
        (0, own_ref),
        (-2, behind_ref),
        (2, ahead_ref),
        (side, partner_ref),
        (-3 * side, far_ref),
        (side - 2, partner_behind_ref),
        (side + 2, partner_ahead_ref),
    )
    for at, ref in candidates:

        @pl.when(offset == at)
        def _(ref=ref):
            pltpu.make_async_copy(ref.at[0], chosen, in_sem).start()

    row = lax.broadcasted_iota(jnp.int32, (GRID, HALF), 0)
    wave_x = lanes((GRID, HALF)).astype(f32)
    wave_y = jnp.where(row < GRID // 2, row, row - GRID).astype(f32)
    wave_sq = wave_y * wave_y + wave_x * wave_x
    inverse_sq = jnp.where(wave_sq > 0, 1.0 / jnp.maximum(wave_sq, 1.0), 0.0)
    along = wave_y * inverse_sq
    cross = wave_x * inverse_sq
    weight = jnp.where(lanes((GRID, HALF)) == 0, 1.0 / 64, 2.0 / 64)
    prior = prior_amplitude / (1.0 + jnp.sqrt(wave_sq) / 8.0)
    decay = 1.0 / (1.0 + time_step * viscosity * wave_sq)
    keeper = ((jnp.abs(wave_y) <= CUT) & (wave_x <= CUT)).astype(f32)
    pull = keeper * (time_step * 64.0 / (GRID * GRID))

    total = tiles_ref[0]
    for at in range(1, PLANE):
        total += tiles_ref[at]
    adapted = jnp.sqrt(jnp.maximum(total, 0.0) / (RING * PLANE) + 1e-06)
    low_lane = lanes((8, HALF)) < LOW

    def spread(part):
        top, bottom = adapted, pltpu.roll(adapted, 128 - LOW, 1)
        if part:
            top = pltpu.roll(adapted, 128 - 2 * LOW, 1)
            bottom = pltpu.roll(adapted, 128 - 3 * LOW, 1)
        return jnp.concatenate(
            [
                jnp.where(low_lane, top, prior[:8]),
                prior[8 : GRID - 8],
                jnp.where(low_lane, bottom, prior[GRID - 8 :]),
            ],
            axis=0,
        )

    scale = [step_size * spread(part) for part in range(2)]

    pltpu.make_async_copy(own_ref.at[0], chosen, in_sem).wait()
    current = [chosen[part] for part in range(2)]
    proposals = []
    for move in range(MOVES):
        proposal = [keep * current[part] + scale[part] * noise_ref[move, 0, part] for part in range(2)]
        proposals.append(proposal)
        taken = accept_ref[move] == 1
        current = [jnp.where(taken, proposal[part], current[part]) for part in range(2)]
    for part in range(2):
        moved_buf[part] = current[part]
    out_copy = pltpu.make_async_copy(moved_buf, moved_ref.at[0], out_sem)
    out_copy.start()

    def load(slot_in, real, imag):
        real_high, real_low = split(real)
        imag_high, imag_low = split(imag)
        for ref, re, im in ((data_high, real_high, imag_high), (data_low, real_low, imag_low)):
            ref[slot_in, :GRID, :HALF] = re
            ref[slot_in, :GRID, HALF:] = -im
            ref[slot_in, GRID:, :HALF] = -im
            ref[slot_in, GRID:, HALF:] = -re

    def synthesize(slot_in, real, imag):
        load(slot_in, real, imag)
        rows = product(across_high[...], across_low[...], data_high[slot_in], data_low[slot_in])
        return product(*split(rows), down_high[...], down_low[...])

    def analyse(slot_in, field):
        rows = product(*split(field), back_high[...], back_low[...])
        load(slot_in, rows[:, :HALF], rows[:, HALF:])
        return [
            product(
                across_high[start : start + BAND],
                across_low[start : start + BAND],
                data_high[slot_in],
                data_low[slot_in],
            )
            for start in (0, GRID - BAND)
        ]

    scores = jnp.zeros((1, MOVES), f32)
    for move in range(MOVES):
        real, imag = proposals[move]
        base = 3 * move
        wr, wi = real * weight, imag * weight
        vort = synthesize(base, wr, wi)
        flow_u = synthesize(base + 1, -along * wi, along * wr)
        flow_v = synthesize(base + 2, cross * wi, -cross * wr)
        flux_u = analyse(base, flow_u * vort)
        flux_v = analyse(base + 1, flow_v * vort)
        push_re, push_im = [], []
        for at, start in enumerate((0, GRID - BAND)):
            kx, ky = (w[start : start + BAND] for w in (wave_x, wave_y))
            factor = pull[start : start + BAND]
            push_re.append(
                factor * (kx * flux_u[at][:, HALF:] + ky * flux_v[at][:, HALF:])
            )
            push_im.append(
                -factor * (kx * flux_u[at][:, :HALF] + ky * flux_v[at][:, :HALF])
            )
        middle = jnp.zeros((GRID - 2 * BAND, HALF), f32)
        change_re = jnp.concatenate([push_re[0], middle, push_re[1]], axis=0)
        change_im = jnp.concatenate([push_im[0], middle, push_im[1]], axis=0)
        final = synthesize(
            base + 2,
            (real + change_re) * decay * weight,
            (imag + change_im) * decay * weight,
        )
        gap = final - observed_ref[...]
        score = jnp.sum(gap * gap, keepdims=True) * (
            1.0 / (2.0 * noise_level * noise_level * GRID * GRID)
        )
        scores = jnp.where(lanes((1, MOVES)) == move, score, scores)
    misfit_ref[...] = scores
    out_copy.wait()


def whole(*shape):
    return pl.BlockSpec(memory_space=pltpu.VMEM)


def body(particles, offspring, noise, accept, observed):
    devices = RING * PLANE
    rings = [[z * PLANE + at for z in range(RING)] for at in range(PLANE)]
    planes = [[z * PLANE + at for at in range(PLANE)] for z in range(RING)]
    vmem, smem = pl.BlockSpec(memory_space=pltpu.VMEM), pl.BlockSpec(memory_space=pltpu.SMEM)
    anywhere = pl.BlockSpec(memory_space=pl.ANY)

    def gather(tiles, groups):
        return lax.all_to_all(tiles, "dom", 0, 0, axis_index_groups=groups, tiled=True)

    def send(value, target):
        pairs = [(i, target(i)) for i in range(devices) if 0 <= target(i) < devices]
        return lax.ppermute(value, "dom", pairs)

    slot_at = lambda: lax.axis_index("dom")
    tile = pl.pallas_call(
        functools.partial(first_kernel, lambda: lax.div(slot_at(), PLANE)),
        grid=(1,),
        in_specs=[
            smem,
            pl.BlockSpec((1, 2, 8, HALF), lambda i: (0, 0, 0, 0)),
            pl.BlockSpec((1, 2, 8, HALF), lambda i: (0, 0, GRID // 8 - 1, 0)),
        ],
        out_specs=pl.BlockSpec((RING, 8, 128), lambda i: (0, 0, 0)),
        out_shape=jax.ShapeDtypeStruct((RING, 8, 128), f32),
        compiler_params=pltpu.CompilerParams(vmem_limit_bytes=2 * 1024 * 1024),
        name="first",
    )(offspring, particles, particles)
    behind = send(particles, lambda i: i + 2)
    ahead = send(particles, lambda i: i - 2)
    partner = send(particles, lambda i: i ^ 1)
    far = send(particles, lambda i: i + 3 if i % 2 else i - 3)
    ring = gather(tile, rings)
    tile = pl.pallas_call(
        second_kernel,
        in_specs=[vmem],
        out_specs=vmem,
        out_shape=jax.ShapeDtypeStruct((PLANE, 8, 128), f32),
        compiler_params=pltpu.CompilerParams(vmem_limit_bytes=2 * 1024 * 1024),
        name="second",
    )(ring)
    partner_behind = send(behind, lambda i: i ^ 1)
    partner_ahead = send(ahead, lambda i: i ^ 1)
    tiles = gather(tile, planes)
    moved, misfit = pl.pallas_call(
        functools.partial(final_kernel, slot_at),
        in_specs=[smem, vmem] + [anywhere] * 7 + [vmem] * 3,
        out_specs=[anywhere, vmem],
        out_shape=[
            jax.ShapeDtypeStruct((1, 2, GRID, HALF), f32),
            jax.ShapeDtypeStruct((1, MOVES), f32),
        ],
        scratch_shapes=[
            pltpu.VMEM((2, GRID, HALF), f32),
            pltpu.VMEM((2, GRID, HALF), f32),
            pltpu.VMEM((6, 2 * GRID, GRID), bf16),
            pltpu.VMEM((6, 2 * GRID, GRID), bf16),
            pltpu.SemaphoreType.DMA,
            pltpu.SemaphoreType.DMA,
        ],
        compiler_params=pltpu.CompilerParams(vmem_limit_bytes=24 * 1024 * 1024),
        name="final",
    )(
        accept.reshape(MOVES),
        tiles,
        particles,
        behind,
        ahead,
        partner,
        far,
        partner_behind,
        partner_ahead,
        noise,
        observed,
        jnp.asarray(tables()),
    )
    return moved, misfit.reshape(MOVES, 1)


def solution(mesh):
    return jax.shard_map(
        body,
        mesh=mesh,
        in_specs=(
            P("dom", None, None, None),
            P("dom"),
            P(None, "dom", None, None, None),
            P(None, "dom"),
            P(),
        ),
        out_specs=(P("dom", None, None, None), P(None, "dom")),
        check_vma=False,
    )
```

time: 999 us -> 69.3 us (0.07); the launches traced: 980 us -> 68.9 us
  blocking collectives: 836 us -> 0 us
  starting transfers between devices: 80.4 us -> 44.2 us
  matrix products: 27.6 us -> 0 us
  local copies, waits for them, and re-layouts: 18.2 us -> 2.18 us
  Pallas kernels: 0 us -> 11.5 us
    psum x1 -> x0, blocking collectives: 725 us -> none  [body(): totals = lax.psum(jnp.sum(low_modes(present_state) ** 2, axis=0), 'dom')]
    unnamed x1 -> x0, blocking collectives: 111 us -> none
    ppermute x18 -> x6, starting transfers between devices: 80.4 us -> 15.4 us  [send(): return lax.ppermute(value, 'dom', pairs)]
    all_to_all x0 -> x2, starting transfers between devices: none -> 28.8 us  [gather(): lax.all_to_all(tiles, 'dom', 0, 0, axis_index_groups=groups, tiled=True)]
    dot_general x19 -> x0, matrix products: 27.6 us -> none  [the longest x4 6.48 us: synthesize(): with_sin = jnp.einsum('ap,bpq->baq', sin_y, stacked, precision=highest)]
    pallas_call x0 -> x3, Pallas kernels: none -> 11.5 us  [the longest x1 10.1 us: body(): pl.pallas_call(functools.partial(final_kernel, slot_at), in_specs=[smem,...]
  transfers between devices with their start and end apart: 18 -> 8, of which waited for: 2 -> 2; matrix products, arithmetic and copies ran while one was open for 2% -> 0% of each run, Pallas kernels for 0% -> 2%
where the time goes in v1:
time: 69.3 us; the launch traced here: 68.9 us
  starting transfers between devices  44.2 us (64%)
  Pallas kernels  11.5 us (17%)
  waiting for transfers between devices  9.58 us (14%)
  local copies, waits for them, and re-layouts  2.18 us (3%)
  between operations  1.43 us (2%)
    all_to_all x2, starting transfers between devices, gather(): lax.all_to_all(tiles, 'dom', 0, 0, axis_index_groups=groups, tiled=True)  28.8 us
    ppermute x6, starting transfers between devices, send(): return lax.ppermute(value, 'dom', pairs)  15.4 us
    pallas_call x1, Pallas kernels, body(): pl.pallas_call(functools.partial(final_kernel, slot_at), in_specs=[smem,...  10.1 us
    all_to_all x2, waiting for transfers between devices, gather(): lax.all_to_all(tiles, 'dom', 0, 0, axis_index_groups=groups, tiled=True)  9.56 us
    unnamed x12, local copies, waits for them, and re-layouts  2.18 us
  transfers between devices with their start and end apart: 8, of which 2 were waited for; matrix products, arithmetic and copies ran while one was open for 0% of the time, Pallas kernels for 2%

profile of v1, /device:TPU:1, one launch (start us, length us, event | category | flops | bytes accessed | tf_op | source)
XLA Modules:
  0.0 68.9 jit_solution(12867856219512568117)
XLA Ops:
  0.6 1.3 %collective-permute-start.1 = (f32[1,2,256,128]{3,2,1,0:T(8,128)}, f32[1,2,256,128]{3,2,1,0:T(8,128)S(1)}, u32[]{:S(2)}, u32[]{:S(2)}) collective-permute-start(f32[1,2,256,128]{3,2,1,0:T(8,128)} %own_ref.1), channel_id=1, source_target_pairs={{2,0},{3,1},{4,2},{5,3},{6,4},{7,5},{8,6},{9,7},{10,8},{11,9},{12,... | collective-permute-start | bytes 786440 | tf_op jit(solution)/shard_map/ppermute | solution.py:274
  1.9 4.6 %collective-permute-start = (f32[1,2,256,128]{3,2,1,0:T(8,128)}, f32[1,2,256,128]{3,2,1,0:T(8,128)S(1)}, u32[]{:S(2)}, u32[]{:S(2)}) collective-permute-start(f32[1,2,256,128]{3,2,1,0:T(8,128)} %own_ref.1), channel_id=1, source_target_pairs={{0,2},{1,3},{2,4},{3,5},{4,6},{5,7},{6,8},{7,9},{8,10},{9,11},{10,... | collective-permute-start | bytes 786440 | tf_op jit(solution)/shard_map/ppermute | solution.py:274
  7.2 0.0 copy-start
  7.2 0.9 %copy-done = f32[1,2,256,128]{3,2,1,0:T(8,128)S(1)} copy-done((f32[1,2,256,128]{3,2,1,0:T(8,128)S(1)}, f32[1,2,256,128]{3,2,1,0:T(8,128)}, u32[]{:S(2)}) %copy-start) | copy-done | bytes 262168
  8.1 0.0 copy-start.1
  8.1 0.0 copy-start.3
  8.1 0.7 %first.1 = f32[16,8,128]{2,1,0:T(8,128)} custom-call(s32[1]{0:T(128)S(6)} %copy.8.offspring_ref, f32[1,2,256,128]{3,2,1,0:T(8,128)S(1)} %copy-done, f32[1,2,256,128]{3,2,1,0:T(8,128)S(1)} %copy-done), custom_call_target="tpu_custom_call" | custom-call | tf_op jit(solution)/shard_map/first/pallas_call | solution.py:277
  8.8 18.6 %all-to-all-start = ((f32[16,8,128]{2,1,0:T(8,128)}), f32[16,8,128]{2,1,0:T(8,128)S(1)}, u32[]{:S(2)}, u32[]{:S(2)}) async-start(f32[16,8,128]{2,1,0:T(8,128)} %first.1), calls=%async_computation | async-start | bytes 131072 | tf_op jit(solution)/shard_map/all_to_all | solution.py:270
  27.5 0.0 copy-done.1
  27.5 0.0 copy-start.4
  27.5 3.3 %collective-permute-start.2 = (f32[1,2,256,128]{3,2,1,0:T(8,128)S(1)}, f32[1,2,256,128]{3,2,1,0:T(8,128)S(1)}, u32[]{:S(2)}, u32[]{:S(2)}) collective-permute-start(f32[1,2,256,128]{3,2,1,0:T(8,128)S(1)} %copy-done.1), channel_id=1, source_target_pairs={{0,1},{1,0},{2,3},{3,2},{4,5},{5,4},{6,7},{7,6},{8,9},{9,8},{10,11... | collective-permute-start | bytes 786440 | tf_op jit(solution)/shard_map/ppermute | solution.py:274
  30.8 1.9 %collective-permute-start.3 = (f32[1,2,256,128]{3,2,1,0:T(8,128)S(1)}, f32[1,2,256,128]{3,2,1,0:T(8,128)S(1)}, u32[]{:S(2)}, u32[]{:S(2)}) collective-permute-start(f32[1,2,256,128]{3,2,1,0:T(8,128)S(1)} %copy-done.1), channel_id=1, source_target_pairs={{1,4},{3,6},{4,1},{5,8},{6,3},{7,10},{8,5},{9,12},{10,7},{11,14},{... | collective-permute-start | bytes 786440 | tf_op jit(solution)/shard_map/ppermute | solution.py:274
  32.7 0.0 collective-permute-done.1.ahead_ref
  32.7 1.9 %collective-permute-start.5 = (f32[1,2,256,128]{3,2,1,0:T(8,128)S(1)}, f32[1,2,256,128]{3,2,1,0:T(8,128)S(1)}, u32[]{:S(2)}, u32[]{:S(2)}) collective-permute-start(f32[1,2,256,128]{3,2,1,0:T(8,128)S(1)} %collective-permute-done.1.ahead_ref), channel_id=1, source_target_pairs={{0,1},{1,0},{2,3},{3,2},{4,5},{5,4},{6,7},{7,6},{8,9},{9,8},{10,11... | collective-permute-start | bytes 786440 | tf_op jit(solution)/shard_map/ppermute | solution.py:274
  34.6 0.0 collective-permute-done.behind_ref
  34.6 2.4 %collective-permute-start.4 = (f32[1,2,256,128]{3,2,1,0:T(8,128)S(1)}, f32[1,2,256,128]{3,2,1,0:T(8,128)S(1)}, u32[]{:S(2)}, u32[]{:S(2)}) collective-permute-start(f32[1,2,256,128]{3,2,1,0:T(8,128)S(1)} %collective-permute-done.behind_ref), channel_id=1, source_target_pairs={{0,1},{1,0},{2,3},{3,2},{4,5},{5,4},{6,7},{7,6},{8,9},{9,8},{10,11... | collective-permute-start | bytes 786440 | tf_op jit(solution)/shard_map/ppermute | solution.py:274
  37.1 2.0 %all-to-all-done.tiles_ref = f32[16,8,128]{2,1,0:T(8,128)S(1)} async-done(((f32[16,8,128]{2,1,0:T(8,128)}), f32[16,8,128]{2,1,0:T(8,128)S(1)}, u32[]{:S(2)}, u32[]{:S(2)}) %all-to-all-start) | async-done | bytes 65568 | tf_op jit(solution)/shard_map/all_to_all | solution.py:270
  39.0 0.7 second.1
  39.7 10.2 %all-to-all-start.1 = ((f32[32,8,128]{2,1,0:T(8,128)}), f32[32,8,128]{2,1,0:T(8,128)S(1)}, u32[]{:S(2)}, u32[]{:S(2)}) async-start(f32[32,8,128]{2,1,0:T(8,128)} %second.1), calls=%async_computation.1 | async-start | bytes 262144 | tf_op jit(solution)/shard_map/all_to_all | solution.py:270
  49.9 0.0 copy-start.5
  49.9 0.0 collective-permute-done.2.partner_ref
  50.0 0.0 collective-permute-done.3.far_ref
  50.0 7.6 %all-to-all-done.1.tiles_ref = f32[32,8,128]{2,1,0:T(8,128)S(1)} async-done(((f32[32,8,128]{2,1,0:T(8,128)}), f32[32,8,128]{2,1,0:T(8,128)S(1)}, u32[]{:S(2)}, u32[]{:S(2)}) %all-to-all-start.1) | async-done | bytes 131104 | tf_op jit(solution)/shard_map/all_to_all | solution.py:270
  57.5 0.0 collective-permute-done.5.partner_ahead_ref
  57.5 0.0 collective-permute-done.4.partner_behind_ref
  57.5 0.0 copy-done.3
  57.5 0.0 copy-done.4
  57.6 0.0 copy-done.5
  57.6 0.0 copy-start.2
  57.6 1.2 %copy-done.2 = bf16[256,2048]{1,0:T(8,128)(2,1)S(1)} copy-done((bf16[256,2048]{1,0:T(8,128)(2,1)S(1)}, bf16[256,2048]{1,0:T(8,128)(2,1)}, u32[]{:S(2)}) %copy-start.2) | copy-done | bytes 1048600
  58.8 10.1 %final.1 = (f32[1,2,256,128]{3,2,1,0:T(8,128)}, f32[1,2]{1,0:T(1,128)}) custom-call(s32[2]{0:T(128)S(1)} %bitcast.2, f32[32,8,128]{2,1,0:T(8,128)S(1)} %all-to-all-done.1.tiles_ref, f32[1,2,256,128]{3,2,1,0:T(8,128)S(1)} %copy-done.1, f32[1,2,256,128]{3,2,1,0:T(8,128)S(1)} %collective-permute-done.behind_ref, ...), custom_call_target="tpu_custom_call" | custom-call | tf_op jit(solution)/shard_map/final/pallas_call | solution.py:306
Async XLA Ops:
  0.6 32.1 %collective-permute-start.1 = (f32[1,2,256,128]{3,2,1,0:T(8,128)}, f32[1,2,256,128]{3,2,1,0:T(8,128)S(1)}, u32[]{:S(2)}, u32[]{:S(2)}) collective-permute-start(f32[1,2,256,128]{3,2,1,0:T(8,128)} %own_ref.1), channel_id=1, source_target_pairs={{2,0},{3,1},{4,2},{5,3},{6,4},{7,5},{8,6},{9,7},{10,8},{11,9},{12,... | collective-permute-start | bytes 786440 | tf_op jit(solution)/shard_map/ppermute | solution.py:274
  1.9 32.7 %collective-permute-start = (f32[1,2,256,128]{3,2,1,0:T(8,128)}, f32[1,2,256,128]{3,2,1,0:T(8,128)S(1)}, u32[]{:S(2)}, u32[]{:S(2)}) collective-permute-start(f32[1,2,256,128]{3,2,1,0:T(8,128)} %own_ref.1), channel_id=1, source_target_pairs={{0,2},{1,3},{2,4},{3,5},{4,6},{5,7},{6,8},{7,9},{8,10},{9,11},{10,... | collective-permute-start | bytes 786440 | tf_op jit(solution)/shard_map/ppermute | solution.py:274
  7.2 1.0 %copy-start = (f32[1,2,256,128]{3,2,1,0:T(8,128)S(1)}, f32[1,2,256,128]{3,2,1,0:T(8,128)}, u32[]{:S(2)}) copy-start(f32[1,2,256,128]{3,2,1,0:T(8,128)} %own_ref.1) | copy-start | bytes 786436
  8.1 19.3 %copy-start.1 = (f32[1,2,256,128]{3,2,1,0:T(8,128)S(1)}, f32[1,2,256,128]{3,2,1,0:T(8,128)}, u32[]{:S(2)}) copy-start(f32[1,2,256,128]{3,2,1,0:T(8,128)} %own_ref.1) | copy-start | bytes 786436
  8.1 49.4 %copy-start.3 = (f32[2,1,2,256,128]{4,3,2,1,0:T(8,128)S(1)}, f32[2,1,2,256,128]{4,3,2,1,0:T(8,128)}, u32[]{:S(2)}) copy-start(f32[2,1,2,256,128]{4,3,2,1,0:T(8,128)} %noise_ref.1) | copy-start | bytes 1572868
  8.8 30.2 %all-to-all-start = ((f32[16,8,128]{2,1,0:T(8,128)}), f32[16,8,128]{2,1,0:T(8,128)S(1)}, u32[]{:S(2)}, u32[]{:S(2)}) async-start(f32[16,8,128]{2,1,0:T(8,128)} %first.1), calls=%async_computation | async-start | bytes 131072 | tf_op jit(solution)/shard_map/all_to_all | solution.py:270
  27.5 30.1 %copy-start.4 = (f32[256,256]{1,0:T(8,128)S(1)}, f32[256,256]{1,0:T(8,128)}, u32[]{:S(2)}) copy-start(f32[256,256]{1,0:T(8,128)} %observed_ref.1) | copy-start | bytes 786436
  27.5 22.5 %collective-permute-start.2 = (f32[1,2,256,128]{3,2,1,0:T(8,128)S(1)}, f32[1,2,256,128]{3,2,1,0:T(8,128)S(1)}, u32[]{:S(2)}, u32[]{:S(2)}) collective-permute-start(f32[1,2,256,128]{3,2,1,0:T(8,128)S(1)} %copy-done.1), channel_id=1, source_target_pairs={{0,1},{1,0},{2,3},{3,2},{4,5},{5,4},{6,7},{7,6},{8,9},{9,8},{10,11... | collective-permute-start | bytes 786440 | tf_op jit(solution)/shard_map/ppermute | solution.py:274
  30.8 19.2 %collective-permute-start.3 = (f32[1,2,256,128]{3,2,1,0:T(8,128)S(1)}, f32[1,2,256,128]{3,2,1,0:T(8,128)S(1)}, u32[]{:S(2)}, u32[]{:S(2)}) collective-permute-start(f32[1,2,256,128]{3,2,1,0:T(8,128)S(1)} %copy-done.1), channel_id=1, source_target_pairs={{1,4},{3,6},{4,1},{5,8},{6,3},{7,10},{8,5},{9,12},{10,7},{11,14},{... | collective-permute-start | bytes 786440 | tf_op jit(solution)/shard_map/ppermute | solution.py:274
  32.7 24.8 %collective-permute-start.5 = (f32[1,2,256,128]{3,2,1,0:T(8,128)S(1)}, f32[1,2,256,128]{3,2,1,0:T(8,128)S(1)}, u32[]{:S(2)}, u32[]{:S(2)}) collective-permute-start(f32[1,2,256,128]{3,2,1,0:T(8,128)S(1)} %collective-permute-done.1.ahead_ref), channel_id=1, source_target_pairs={{0,1},{1,0},{2,3},{3,2},{4,5},{5,4},{6,7},{7,6},{8,9},{9,8},{10,11... | collective-permute-start | bytes 786440 | tf_op jit(solution)/shard_map/ppermute | solution.py:274
  34.6 22.9 %collective-permute-start.4 = (f32[1,2,256,128]{3,2,1,0:T(8,128)S(1)}, f32[1,2,256,128]{3,2,1,0:T(8,128)S(1)}, u32[]{:S(2)}, u32[]{:S(2)}) collective-permute-start(f32[1,2,256,128]{3,2,1,0:T(8,128)S(1)} %collective-permute-done.behind_ref), channel_id=1, source_target_pairs={{0,1},{1,0},{2,3},{3,2},{4,5},{5,4},{6,7},{7,6},{8,9},{9,8},{10,11... | collective-permute-start | bytes 786440 | tf_op jit(solution)/shard_map/ppermute | solution.py:274
  39.7 17.8 %all-to-all-start.1 = ((f32[32,8,128]{2,1,0:T(8,128)}), f32[32,8,128]{2,1,0:T(8,128)S(1)}, u32[]{:S(2)}, u32[]{:S(2)}) async-start(f32[32,8,128]{2,1,0:T(8,128)} %second.1), calls=%async_computation.1 | async-start | bytes 262144 | tf_op jit(solution)/shard_map/all_to_all | solution.py:270
  49.9 7.6 %copy-start.5 = (s32[2,1]{0,1:T(1,128)S(1)}, s32[2,1]{0,1:T(1,128)}, u32[]{:S(2)}) copy-start(s32[2,1]{0,1:T(1,128)} %param.9) | copy-start | bytes 28
  57.6 1.2 %copy-start.2 = (bf16[256,2048]{1,0:T(8,128)(2,1)S(1)}, bf16[256,2048]{1,0:T(8,128)(2,1)}, u32[]{:S(2)}) copy-start(bf16[256,2048]{1,0:T(8,128)(2,1)} %constant.2.clone.table_ref) | copy-start | bytes 3145732

commit v2 on v1

--- a/solution.py
+++ b/solution.py
@@ -41,10 +41,12 @@
     index = np.arange(GRID)
     phase = (index[:, None] * index[None, :] % GRID) * (2.0 * np.pi / GRID)
     cos, sin = np.cos(phase), np.sin(phase)
-    across = np.concatenate([cos, sin], axis=1)
-    down = np.concatenate([cos[:HALF], sin[:HALF]], axis=0)
+    turned = sin[:HALF].copy()
+    turned[0] = 1.0 - 2.0 * (index % 2)
+    across = np.concatenate([cos[:HALF], turned], axis=0)
+    down = np.concatenate([cos[:HALF], -sin[:HALF]], axis=0)
     back = np.concatenate([cos[:, :HALF], sin[:, :HALF]], axis=1)
-    parts = split_table(across) + split_table(down) + split_table(back)
+    parts = [half for t in (across, down, back, across.T) for half in split_table(t)]
     return np.concatenate(parts, axis=1)
 
 
@@ -52,10 +54,10 @@
     return lax.broadcasted_iota(jnp.int32, shape, len(shape) - 1)
 
 
-def first_kernel(ring_at, offspring_ref, top_ref, bottom_ref, tile_ref):
+def first_kernel(plane_at, offspring_ref, top_ref, bottom_ref, tile_ref):
     count = offspring_ref[0].astype(f32)
     lane = lanes((8, 128))
-    tile = jnp.where(lane == COUNTS + ring_at(), count, 0.0)
+    tile = jnp.where(lane == COUNTS + plane_at(), count, 0.0)
     for part in range(2):
         for side, ref in enumerate((top_ref, bottom_ref)):
             low = jnp.where(lane < LOW, ref[0, part], 0.0)
@@ -67,7 +69,7 @@
 
 def second_kernel(tiles_ref, tile_ref):
     total = tiles_ref[0]
-    for at in range(1, RING):
+    for at in range(1, PLANE):
         total += tiles_ref[at]
     tile_ref[...] = jnp.broadcast_to(total[None], tile_ref.shape)
 
@@ -75,6 +77,16 @@
 def split(value):
     high = value.astype(bf16)
     return high, (value - high.astype(f32)).astype(bf16)
+
+
+def backwards(rows):
+    count, width = rows.shape
+    groups = pltpu.roll(rows, count - 1, 0).reshape(count // 8, 8, width)
+    sub = lax.broadcasted_iota(jnp.int32, groups.shape, 1)
+    for step in (4, 2, 1):
+        up, lower = pltpu.roll(groups, 8 - step, 1), pltpu.roll(groups, step, 1)
+        groups = jnp.where(lax.rem(lax.div(sub, step), 2) == 0, up, lower)
+    return jnp.concatenate([groups[i] for i in range(count // 8)][::-1], axis=0)
 
 
 def product(left_high, left_low, right_high, right_low):
@@ -104,21 +116,25 @@
     moved_buf,
     data_high,
     data_low,
+    table_buf,
+    table_sem,
     in_sem,
     out_sem,
 ):
-    across_high, across_low, down_high, down_low, back_high, back_low = (
-        table_ref.at[:, start : start + size]
-        for start, size in ((0, 512), (512, 512), (1024, 256), (1280, 256), (1536, 256), (1792, 256))
+    table_copy = pltpu.make_async_copy(table_ref, table_buf, table_sem)
+    table_copy.start()
+    across, down, back, gather = (
+        [table_buf.at[:, start : start + GRID] for start in (at, at + GRID)]
+        for at in range(0, 8 * GRID, 2 * GRID)
     )
     slot = slot_at()
     odd = lax.rem(slot, 2)
 
     counts = tiles_ref[:, 0, :]
-    lane = lanes((PLANE, 128))
-    plane_at = lax.broadcasted_iota(jnp.int32, (PLANE, 128), 0)
-    place = (lane - COUNTS) * PLANE + plane_at
-    counted = (lane >= COUNTS) & (lane < COUNTS + RING)
+    lane = lanes((RING, 128))
+    ring_at = lax.broadcasted_iota(jnp.int32, (RING, 128), 0)
+    place = ring_at * PLANE + lane - COUNTS
+    counted = (lane >= COUNTS) & (lane < COUNTS + PLANE)
     offset = jnp.full((1, 1), -3, jnp.int32)
     for distance in range(-3, 4):
         ends = jnp.sum(
@@ -157,7 +173,7 @@
     pull = keeper * (time_step * 64.0 / (GRID * GRID))
 
     total = tiles_ref[0]
-    for at in range(1, PLANE):
+    for at in range(1, RING):
         total += tiles_ref[at]
     adapted = jnp.sqrt(jnp.maximum(total, 0.0) / (RING * PLANE) + 1e-06)
     low_lane = lanes((8, HALF)) < LOW
@@ -191,32 +207,61 @@
     out_copy = pltpu.make_async_copy(moved_buf, moved_ref.at[0], out_sem)
     out_copy.start()
 
-    def load(slot_in, real, imag):
-        real_high, real_low = split(real)
-        imag_high, imag_low = split(imag)
-        for ref, re, im in ((data_high, real_high, imag_high), (data_low, real_low, imag_low)):
-            ref[slot_in, :GRID, :HALF] = re
-            ref[slot_in, :GRID, HALF:] = -im
-            ref[slot_in, GRID:, :HALF] = -im
-            ref[slot_in, GRID:, HALF:] = -re
-
-    def synthesize(slot_in, real, imag):
-        load(slot_in, real, imag)
-        rows = product(across_high[...], across_low[...], data_high[slot_in], data_low[slot_in])
-        return product(*split(rows), down_high[...], down_low[...])
-
-    def analyse(slot_in, field):
-        rows = product(*split(field), back_high[...], back_low[...])
-        load(slot_in, rows[:, :HALF], rows[:, HALF:])
+    table_copy.wait()
+
+    def synthesize(at, real, imag):
+        for half, value in enumerate((real, imag)):
+            high, low = split(value)
+            data_high[at, :, half * HALF : (half + 1) * HALF] = high
+            data_low[at, :, half * HALF : (half + 1) * HALF] = low
+        both = product(across[0][...], across[1][...], data_high[at], data_low[at])
+        even_re, even_im = both[:HALF, :HALF], both[:HALF, HALF:]
+        odd_re, odd_im = both[HALF:, :HALF], both[HALF:, HALF:]
+        rows_re = jnp.concatenate(
+            [
+                jnp.where(first_row, even_re, even_re - odd_im),
+                jnp.where(first_row, odd_re, even_re + odd_im),
+            ],
+            axis=0,
+        )
+        rows_im = jnp.concatenate(
+            [
+                jnp.where(first_row, even_im, even_im + odd_re),
+                jnp.where(first_row, odd_im, even_im - odd_re),
+            ],
+            axis=0,
+        )
+        rows = jnp.concatenate([rows_re, rows_im], axis=1)
+        return product(*split(rows), down[0][...], down[1][...])
+
+    def analyse(at, field):
+        rows = product(*split(field), back[0][...], back[1][...])
+        plus_c, plus_s = rows[:HALF, :HALF], rows[:HALF, HALF:]
+        minus_c, minus_s = rows[HALF:, :HALF], rows[HALF:, HALF:]
+        quarters = (
+            (0, 0, jnp.where(first_row, plus_c, plus_c + minus_c)),
+            (0, HALF, -jnp.where(first_row, plus_s, plus_s + minus_s)),
+            (HALF, 0, jnp.where(first_row, minus_c, minus_s - plus_s)),
+            (HALF, HALF, jnp.where(first_row, -minus_s, minus_c - plus_c)),
+        )
+        for row, column, value in quarters:
+            high, low = split(value)
+            data_high[at, row : row + HALF, column : column + HALF] = high
+            data_low[at, row : row + HALF, column : column + HALF] = low
         return [
             product(
-                across_high[start : start + BAND],
-                across_low[start : start + BAND],
-                data_high[slot_in],
-                data_low[slot_in],
+                gather[0][start : start + BAND],
+                gather[1][start : start + BAND],
+                data_high[at],
+                data_low[at],
             )
             for start in (0, GRID - BAND)
         ]
+
+    first_row = lax.broadcasted_iota(jnp.int32, (HALF, HALF), 0) == 0
+    target = jnp.concatenate(
+        [observed_ref[:HALF], backwards(observed_ref[HALF:])], axis=0
+    )
 
     scores = jnp.zeros((1, MOVES), f32)
     for move in range(MOVES):
@@ -246,17 +291,13 @@
             (real + change_re) * decay * weight,
             (imag + change_im) * decay * weight,
         )
-        gap = final - observed_ref[...]
+        gap = final - target
         score = jnp.sum(gap * gap, keepdims=True) * (
             1.0 / (2.0 * noise_level * noise_level * GRID * GRID)
         )
         scores = jnp.where(lanes((1, MOVES)) == move, score, scores)
     misfit_ref[...] = scores
     out_copy.wait()
-
-
-def whole(*shape):
-    return pl.BlockSpec(memory_space=pltpu.VMEM)
 
 
 def body(particles, offspring, noise, accept, observed):
@@ -275,15 +316,15 @@
 
     slot_at = lambda: lax.axis_index("dom")
     tile = pl.pallas_call(
-        functools.partial(first_kernel, lambda: lax.div(slot_at(), PLANE)),
+        functools.partial(first_kernel, lambda: lax.rem(slot_at(), PLANE)),
         grid=(1,),
         in_specs=[
             smem,
             pl.BlockSpec((1, 2, 8, HALF), lambda i: (0, 0, 0, 0)),
             pl.BlockSpec((1, 2, 8, HALF), lambda i: (0, 0, GRID // 8 - 1, 0)),
         ],
-        out_specs=pl.BlockSpec((RING, 8, 128), lambda i: (0, 0, 0)),
-        out_shape=jax.ShapeDtypeStruct((RING, 8, 128), f32),
+        out_specs=pl.BlockSpec((PLANE, 8, 128), lambda i: (0, 0, 0)),
+        out_shape=jax.ShapeDtypeStruct((PLANE, 8, 128), f32),
         compiler_params=pltpu.CompilerParams(vmem_limit_bytes=2 * 1024 * 1024),
         name="first",
     )(offspring, particles, particles)
@@ -291,21 +332,21 @@
     ahead = send(particles, lambda i: i - 2)
     partner = send(particles, lambda i: i ^ 1)
     far = send(particles, lambda i: i + 3 if i % 2 else i - 3)
-    ring = gather(tile, rings)
+    plane = gather(tile, planes)
     tile = pl.pallas_call(
         second_kernel,
         in_specs=[vmem],
         out_specs=vmem,
-        out_shape=jax.ShapeDtypeStruct((PLANE, 8, 128), f32),
+        out_shape=jax.ShapeDtypeStruct((RING, 8, 128), f32),
         compiler_params=pltpu.CompilerParams(vmem_limit_bytes=2 * 1024 * 1024),
         name="second",
-    )(ring)
+    )(plane)
     partner_behind = send(behind, lambda i: i ^ 1)
     partner_ahead = send(ahead, lambda i: i ^ 1)
-    tiles = gather(tile, planes)
+    tiles = gather(tile, rings)
     moved, misfit = pl.pallas_call(
         functools.partial(final_kernel, slot_at),
-        in_specs=[smem, vmem] + [anywhere] * 7 + [vmem] * 3,
+        in_specs=[smem, vmem] + [anywhere] * 7 + [vmem] * 2 + [anywhere],
         out_specs=[anywhere, vmem],
         out_shape=[
             jax.ShapeDtypeStruct((1, 2, GRID, HALF), f32),
@@ -314,8 +355,10 @@
         scratch_shapes=[
             pltpu.VMEM((2, GRID, HALF), f32),
             pltpu.VMEM((2, GRID, HALF), f32),
-            pltpu.VMEM((6, 2 * GRID, GRID), bf16),
-            pltpu.VMEM((6, 2 * GRID, GRID), bf16),
+            pltpu.VMEM((6, GRID, GRID), bf16),
+            pltpu.VMEM((6, GRID, GRID), bf16),
+            pltpu.VMEM((GRID, 8 * GRID), bf16),
+            pltpu.SemaphoreType.DMA,
             pltpu.SemaphoreType.DMA,
             pltpu.SemaphoreType.DMA,
         ],
@@ -333,7 +376,7 @@
         partner_ahead,
         noise,
         observed,
-        jnp.asarray(tables()),
+        pltpu.with_memory_space_constraint(jnp.asarray(tables()), pltpu.HBM),
     )
     return moved, misfit.reshape(MOVES, 1)
 

time: 69.3 us -> 70 us (1.010)
  Pallas kernels: 11.5 us -> 8.18 us
  starting transfers between devices: 44.2 us -> 47.5 us
  waiting for transfers between devices: 9.58 us -> 11.6 us
  local copies, waits for them, and re-layouts: 2.18 us -> 0.96 us
    pallas_call x1, Pallas kernels: 10.1 us -> 6.77 us  [body(): pl.pallas_call(functools.partial(final_kernel, slot_at), in_specs=[smem,...]
    all_to_all x2, waiting for transfers between devices: 9.56 us -> 11.5 us  [gather(): lax.all_to_all(tiles, 'dom', 0, 0, axis_index_groups=groups, tiled=True)]
    ppermute x6, starting transfers between devices: 15.4 us -> 17.3 us  [send(): return lax.ppermute(value, 'dom', pairs)]
    all_to_all x2, starting transfers between devices: 28.8 us -> 30.2 us  [gather(): lax.all_to_all(tiles, 'dom', 0, 0, axis_index_groups=groups, tiled=True)]
    unnamed x12 -> x10, local copies, waits for them, and re-layouts: 2.18 us -> 0.96 us
  transfers between devices with their start and end apart: 8 -> 8, of which waited for: 2 -> 1; matrix products, arithmetic and copies ran while one was open for 0% -> 0% of each run, Pallas kernels for 2% -> 2%
where the time goes in v2:
time: 70 us; the launch traced here: 69.6 us
  starting transfers between devices  47.5 us (68%)
  waiting for transfers between devices  11.6 us (17%)
  Pallas kernels  8.18 us (12%)
  between operations  1.43 us (2%)
  local copies, waits for them, and re-layouts  0.96 us (1%)
    all_to_all x2, starting transfers between devices, gather(): lax.all_to_all(tiles, 'dom', 0, 0, axis_index_groups=groups, tiled=True)  30.2 us
    ppermute x6, starting transfers between devices, send(): return lax.ppermute(value, 'dom', pairs)  17.3 us
    all_to_all x2, waiting for transfers between devices, gather(): lax.all_to_all(tiles, 'dom', 0, 0, axis_index_groups=groups, tiled=True)  11.5 us
    pallas_call x1, Pallas kernels, body(): pl.pallas_call(functools.partial(final_kernel, slot_at), in_specs=[smem,...  6.77 us
  transfers between devices with their start and end apart: 8, of which 1 were waited for; matrix products, arithmetic and copies ran while one was open for 0% of the time, Pallas kernels for 2%

profile of v2, /device:TPU:1, one launch (start us, length us, event | category | flops | bytes accessed | tf_op | source)
XLA Modules:
  0.0 69.6 jit_solution(2422597393046507683)
XLA Ops:
  0.6 1.3 %collective-permute-start.1 = (f32[1,2,256,128]{3,2,1,0:T(8,128)}, f32[1,2,256,128]{3,2,1,0:T(8,128)S(1)}, u32[]{:S(2)}, u32[]{:S(2)}) collective-permute-start(f32[1,2,256,128]{3,2,1,0:T(8,128)} %own_ref.1), channel_id=1, source_target_pairs={{2,0},{3,1},{4,2},{5,3},{6,4},{7,5},{8,6},{9,7},{10,8},{11,9},{12,... | collective-permute-start | bytes 786440 | tf_op jit(solution)/shard_map/ppermute | solution.py:315
  1.9 4.6 %collective-permute-start = (f32[1,2,256,128]{3,2,1,0:T(8,128)}, f32[1,2,256,128]{3,2,1,0:T(8,128)S(1)}, u32[]{:S(2)}, u32[]{:S(2)}) collective-permute-start(f32[1,2,256,128]{3,2,1,0:T(8,128)} %own_ref.1), channel_id=1, source_target_pairs={{0,2},{1,3},{2,4},{3,5},{4,6},{5,7},{6,8},{7,9},{8,10},{9,11},{10,... | collective-permute-start | bytes 786440 | tf_op jit(solution)/shard_map/ppermute | solution.py:315
  7.2 0.0 copy-start
  7.2 0.9 %copy-done = f32[1,2,256,128]{3,2,1,0:T(8,128)S(1)} copy-done((f32[1,2,256,128]{3,2,1,0:T(8,128)S(1)}, f32[1,2,256,128]{3,2,1,0:T(8,128)}, u32[]{:S(2)}) %copy-start) | copy-done | bytes 262168
  8.1 0.0 copy-start.2
  8.1 0.7 %first.1 = f32[32,8,128]{2,1,0:T(8,128)} custom-call(s32[1]{0:T(128)S(6)} %copy.8.offspring_ref, f32[1,2,256,128]{3,2,1,0:T(8,128)S(1)} %copy-done, f32[1,2,256,128]{3,2,1,0:T(8,128)S(1)} %copy-done), custom_call_target="tpu_custom_call" | custom-call | tf_op jit(solution)/shard_map/first/pallas_call | solution.py:318
  8.9 0.0 copy-start.1
  8.9 0.0 copy-start.3
  8.9 12.5 %all-to-all-start = ((f32[32,8,128]{2,1,0:T(8,128)}), f32[32,8,128]{2,1,0:T(8,128)S(1)}, u32[]{:S(2)}, u32[]{:S(2)}) async-start(f32[32,8,128]{2,1,0:T(8,128)} %first.1), calls=%async_computation | async-start | bytes 262144 | tf_op jit(solution)/shard_map/all_to_all | solution.py:311
  21.3 0.0 copy-done.1
  21.3 2.1 %collective-permute-start.2 = (f32[1,2,256,128]{3,2,1,0:T(8,128)S(1)}, f32[1,2,256,128]{3,2,1,0:T(8,128)S(1)}, u32[]{:S(2)}, u32[]{:S(2)}) collective-permute-start(f32[1,2,256,128]{3,2,1,0:T(8,128)S(1)} %copy-done.1), channel_id=1, source_target_pairs={{0,1},{1,0},{2,3},{3,2},{4,5},{5,4},{6,7},{7,6},{8,9},{9,8},{10,11... | collective-permute-start | bytes 786440 | tf_op jit(solution)/shard_map/ppermute | solution.py:315
  23.5 4.9 %collective-permute-start.3 = (f32[1,2,256,128]{3,2,1,0:T(8,128)S(1)}, f32[1,2,256,128]{3,2,1,0:T(8,128)S(1)}, u32[]{:S(2)}, u32[]{:S(2)}) collective-permute-start(f32[1,2,256,128]{3,2,1,0:T(8,128)S(1)} %copy-done.1), channel_id=1, source_target_pairs={{1,4},{3,6},{4,1},{5,8},{6,3},{7,10},{8,5},{9,12},{10,7},{11,14},{... | collective-permute-start | bytes 786440 | tf_op jit(solution)/shard_map/ppermute | solution.py:315
  28.4 0.0 collective-permute-done.1.ahead_ref
  28.4 1.9 %collective-permute-start.5 = (f32[1,2,256,128]{3,2,1,0:T(8,128)S(1)}, f32[1,2,256,128]{3,2,1,0:T(8,128)S(1)}, u32[]{:S(2)}, u32[]{:S(2)}) collective-permute-start(f32[1,2,256,128]{3,2,1,0:T(8,128)S(1)} %collective-permute-done.1.ahead_ref), channel_id=1, source_target_pairs={{0,1},{1,0},{2,3},{3,2},{4,5},{5,4},{6,7},{7,6},{8,9},{9,8},{10,11... | collective-permute-start | bytes 786440 | tf_op jit(solution)/shard_map/ppermute | solution.py:315
  30.4 0.0 collective-permute-done.behind_ref
  30.4 2.4 %collective-permute-start.4 = (f32[1,2,256,128]{3,2,1,0:T(8,128)S(1)}, f32[1,2,256,128]{3,2,1,0:T(8,128)S(1)}, u32[]{:S(2)}, u32[]{:S(2)}) collective-permute-start(f32[1,2,256,128]{3,2,1,0:T(8,128)S(1)} %collective-permute-done.behind_ref), channel_id=1, source_target_pairs={{0,1},{1,0},{2,3},{3,2},{4,5},{5,4},{6,7},{7,6},{8,9},{9,8},{10,11... | collective-permute-start | bytes 786440 | tf_op jit(solution)/shard_map/ppermute | solution.py:315
  32.8 0.0 all-to-all-done.tiles_ref
  32.8 0.7 second.1
  33.5 17.7 %all-to-all-start.1 = ((f32[16,8,128]{2,1,0:T(8,128)}), f32[16,8,128]{2,1,0:T(8,128)S(1)}, u32[]{:S(2)}, u32[]{:S(2)}) async-start(f32[16,8,128]{2,1,0:T(8,128)} %second.1), calls=%async_computation.1 | async-start | bytes 131072 | tf_op jit(solution)/shard_map/all_to_all | solution.py:311
  51.2 0.0 copy-start.4
  51.2 0.0 collective-permute-done.2.partner_ref
  51.2 0.0 collective-permute-done.3.far_ref
  51.3 11.5 %all-to-all-done.1.tiles_ref = f32[16,8,128]{2,1,0:T(8,128)S(1)} async-done(((f32[16,8,128]{2,1,0:T(8,128)}), f32[16,8,128]{2,1,0:T(8,128)S(1)}, u32[]{:S(2)}, u32[]{:S(2)}) %all-to-all-start.1) | async-done | bytes 65568 | tf_op jit(solution)/shard_map/all_to_all | solution.py:311
  62.8 0.0 collective-permute-done.5.partner_ahead_ref
  62.8 0.0 collective-permute-done.4.partner_behind_ref
  62.8 0.0 copy-done.2
  62.8 0.0 copy-done.3
  62.8 0.0 copy-done.4
  62.8 6.8 %final.1 = (f32[1,2,256,128]{3,2,1,0:T(8,128)}, f32[1,2]{1,0:T(1,128)}) custom-call(s32[2]{0:T(128)S(1)} %bitcast.2, f32[16,8,128]{2,1,0:T(8,128)S(1)} %all-to-all-done.1.tiles_ref, f32[1,2,256,128]{3,2,1,0:T(8,128)S(1)} %copy-done.1, f32[1,2,256,128]{3,2,1,0:T(8,128)S(1)} %collective-permute-done.behind_ref, ...), custom_call_target="tpu_custom_call" | custom-call | tf_op jit(solution)/shard_map/final/pallas_call | solution.py:347
Async XLA Ops:
  0.6 27.8 %collective-permute-start.1 = (f32[1,2,256,128]{3,2,1,0:T(8,128)}, f32[1,2,256,128]{3,2,1,0:T(8,128)S(1)}, u32[]{:S(2)}, u32[]{:S(2)}) collective-permute-start(f32[1,2,256,128]{3,2,1,0:T(8,128)} %own_ref.1), channel_id=1, source_target_pairs={{2,0},{3,1},{4,2},{5,3},{6,4},{7,5},{8,6},{9,7},{10,8},{11,9},{12,... | collective-permute-start | bytes 786440 | tf_op jit(solution)/shard_map/ppermute | solution.py:315
  1.9 28.4 %collective-permute-start = (f32[1,2,256,128]{3,2,1,0:T(8,128)}, f32[1,2,256,128]{3,2,1,0:T(8,128)S(1)}, u32[]{:S(2)}, u32[]{:S(2)}) collective-permute-start(f32[1,2,256,128]{3,2,1,0:T(8,128)} %own_ref.1), channel_id=1, source_target_pairs={{0,2},{1,3},{2,4},{3,5},{4,6},{5,7},{6,8},{7,9},{8,10},{9,11},{10,... | collective-permute-start | bytes 786440 | tf_op jit(solution)/shard_map/ppermute | solution.py:315
  7.2 1.0 %copy-start = (f32[1,2,256,128]{3,2,1,0:T(8,128)S(1)}, f32[1,2,256,128]{3,2,1,0:T(8,128)}, u32[]{:S(2)}) copy-start(f32[1,2,256,128]{3,2,1,0:T(8,128)} %own_ref.1) | copy-start | bytes 786436
  8.1 54.7 %copy-start.2 = (f32[2,1,2,256,128]{4,3,2,1,0:T(8,128)S(1)}, f32[2,1,2,256,128]{4,3,2,1,0:T(8,128)}, u32[]{:S(2)}) copy-start(f32[2,1,2,256,128]{4,3,2,1,0:T(8,128)} %noise_ref.1) | copy-start | bytes 1572868
  8.9 12.5 %copy-start.1 = (f32[1,2,256,128]{3,2,1,0:T(8,128)S(1)}, f32[1,2,256,128]{3,2,1,0:T(8,128)}, u32[]{:S(2)}) copy-start(f32[1,2,256,128]{3,2,1,0:T(8,128)} %own_ref.1) | copy-start | bytes 786436
  8.9 53.9 %copy-start.3 = (f32[256,256]{1,0:T(8,128)S(1)}, f32[256,256]{1,0:T(8,128)}, u32[]{:S(2)}) copy-start(f32[256,256]{1,0:T(8,128)} %observed_ref.1) | copy-start | bytes 786436
  8.9 23.9 %all-to-all-start = ((f32[32,8,128]{2,1,0:T(8,128)}), f32[32,8,128]{2,1,0:T(8,128)S(1)}, u32[]{:S(2)}, u32[]{:S(2)}) async-start(f32[32,8,128]{2,1,0:T(8,128)} %first.1), calls=%async_computation | async-start | bytes 262144 | tf_op jit(solution)/shard_map/all_to_all | solution.py:311
  21.3 29.9 %collective-permute-start.2 = (f32[1,2,256,128]{3,2,1,0:T(8,128)S(1)}, f32[1,2,256,128]{3,2,1,0:T(8,128)S(1)}, u32[]{:S(2)}, u32[]{:S(2)}) collective-permute-start(f32[1,2,256,128]{3,2,1,0:T(8,128)S(1)} %copy-done.1), channel_id=1, source_target_pairs={{0,1},{1,0},{2,3},{3,2},{4,5},{5,4},{6,7},{7,6},{8,9},{9,8},{10,11... | collective-permute-start | bytes 786440 | tf_op jit(solution)/shard_map/ppermute | solution.py:315
  23.5 27.8 %collective-permute-start.3 = (f32[1,2,256,128]{3,2,1,0:T(8,128)S(1)}, f32[1,2,256,128]{3,2,1,0:T(8,128)S(1)}, u32[]{:S(2)}, u32[]{:S(2)}) collective-permute-start(f32[1,2,256,128]{3,2,1,0:T(8,128)S(1)} %copy-done.1), channel_id=1, source_target_pairs={{1,4},{3,6},{4,1},{5,8},{6,3},{7,10},{8,5},{9,12},{10,7},{11,14},{... | collective-permute-start | bytes 786440 | tf_op jit(solution)/shard_map/ppermute | solution.py:315
  28.4 34.4 %collective-permute-start.5 = (f32[1,2,256,128]{3,2,1,0:T(8,128)S(1)}, f32[1,2,256,128]{3,2,1,0:T(8,128)S(1)}, u32[]{:S(2)}, u32[]{:S(2)}) collective-permute-start(f32[1,2,256,128]{3,2,1,0:T(8,128)S(1)} %collective-permute-done.1.ahead_ref), channel_id=1, source_target_pairs={{0,1},{1,0},{2,3},{3,2},{4,5},{5,4},{6,7},{7,6},{8,9},{9,8},{10,11... | collective-permute-start | bytes 786440 | tf_op jit(solution)/shard_map/ppermute | solution.py:315
  30.4 32.4 %collective-permute-start.4 = (f32[1,2,256,128]{3,2,1,0:T(8,128)S(1)}, f32[1,2,256,128]{3,2,1,0:T(8,128)S(1)}, u32[]{:S(2)}, u32[]{:S(2)}) collective-permute-start(f32[1,2,256,128]{3,2,1,0:T(8,128)S(1)} %collective-permute-done.behind_ref), channel_id=1, source_target_pairs={{0,1},{1,0},{2,3},{3,2},{4,5},{5,4},{6,7},{7,6},{8,9},{9,8},{10,11... | collective-permute-start | bytes 786440 | tf_op jit(solution)/shard_map/ppermute | solution.py:315
  33.5 29.3 %all-to-all-start.1 = ((f32[16,8,128]{2,1,0:T(8,128)}), f32[16,8,128]{2,1,0:T(8,128)S(1)}, u32[]{:S(2)}, u32[]{:S(2)}) async-start(f32[16,8,128]{2,1,0:T(8,128)} %second.1), calls=%async_computation.1 | async-start | bytes 131072 | tf_op jit(solution)/shard_map/all_to_all | solution.py:311
  51.2 11.6 %copy-start.4 = (s32[2,1]{0,1:T(1,128)S(1)}, s32[2,1]{0,1:T(1,128)}, u32[]{:S(2)}) copy-start(s32[2,1]{0,1:T(1,128)} %param.9) | copy-start | bytes 28

commit v3 on v2

--- a/solution.py
+++ b/solution.py
@@ -54,13 +54,23 @@
     return lax.broadcasted_iota(jnp.int32, shape, len(shape) - 1)
 
 
-def first_kernel(plane_at, offspring_ref, top_ref, bottom_ref, tile_ref):
-    count = offspring_ref[0].astype(f32)
+def first_kernel(plane_at, offspring_ref, particle_ref, tile_ref, low_buf, sems):
+    copies = [
+        pltpu.make_async_copy(
+            particle_ref.at[0, :, pl.ds(start, 8)], low_buf.at[side], sems.at[side]
+        )
+        for side, start in enumerate((0, GRID - 8))
+    ]
+    for copy in copies:
+        copy.start()
+    for copy in copies:
+        copy.wait()
+    count = offspring_ref[...]
     lane = lanes((8, 128))
     tile = jnp.where(lane == COUNTS + plane_at(), count, 0.0)
     for part in range(2):
-        for side, ref in enumerate((top_ref, bottom_ref)):
-            low = jnp.where(lane < LOW, ref[0, part], 0.0)
+        for side in range(2):
+            low = jnp.where(lane < LOW, low_buf[side, part], 0.0)
             square = count * (low * low)
             shift = (2 * part + side) * LOW
             tile += pltpu.roll(square, shift, 1) if shift else square
@@ -117,12 +127,16 @@
     data_high,
     data_low,
     table_buf,
+    observed_buf,
     table_sem,
+    observed_sem,
     in_sem,
     out_sem,
 ):
     table_copy = pltpu.make_async_copy(table_ref, table_buf, table_sem)
     table_copy.start()
+    observed_copy = pltpu.make_async_copy(observed_ref, observed_buf, observed_sem)
+    observed_copy.start()
     across, down, back, gather = (
         [table_buf.at[:, start : start + GRID] for start in (at, at + GRID)]
         for at in range(0, 8 * GRID, 2 * GRID)
@@ -208,6 +222,7 @@
     out_copy.start()
 
     table_copy.wait()
+    observed_copy.wait()
 
     def synthesize(at, real, imag):
         for half, value in enumerate((real, imag)):
@@ -260,7 +275,7 @@
 
     first_row = lax.broadcasted_iota(jnp.int32, (HALF, HALF), 0) == 0
     target = jnp.concatenate(
-        [observed_ref[:HALF], backwards(observed_ref[HALF:])], axis=0
+        [observed_buf[:HALF], backwards(observed_buf[HALF:])], axis=0
     )
 
     scores = jnp.zeros((1, MOVES), f32)
@@ -317,17 +332,19 @@
     slot_at = lambda: lax.axis_index("dom")
     tile = pl.pallas_call(
         functools.partial(first_kernel, lambda: lax.rem(slot_at(), PLANE)),
-        grid=(1,),
-        in_specs=[
-            smem,
-            pl.BlockSpec((1, 2, 8, HALF), lambda i: (0, 0, 0, 0)),
-            pl.BlockSpec((1, 2, 8, HALF), lambda i: (0, 0, GRID // 8 - 1, 0)),
+        in_specs=[vmem, anywhere],
+        out_specs=vmem,
+        out_shape=jax.ShapeDtypeStruct((PLANE, 8, 128), f32),
+        scratch_shapes=[
+            pltpu.VMEM((2, 2, 8, HALF), f32),
+            pltpu.SemaphoreType.DMA((2,)),
         ],
-        out_specs=pl.BlockSpec((PLANE, 8, 128), lambda i: (0, 0, 0)),
-        out_shape=jax.ShapeDtypeStruct((PLANE, 8, 128), f32),
         compiler_params=pltpu.CompilerParams(vmem_limit_bytes=2 * 1024 * 1024),
         name="first",
-    )(offspring, particles, particles)
+    )(
+        jnp.broadcast_to(offspring.astype(f32), (8, 128)),
+        pltpu.with_memory_space_constraint(particles, pltpu.HBM),
+    )
     behind = send(particles, lambda i: i + 2)
     ahead = send(particles, lambda i: i - 2)
     partner = send(particles, lambda i: i ^ 1)
@@ -346,7 +363,7 @@
     tiles = gather(tile, rings)
     moved, misfit = pl.pallas_call(
         functools.partial(final_kernel, slot_at),
-        in_specs=[smem, vmem] + [anywhere] * 7 + [vmem] * 2 + [anywhere],
+        in_specs=[smem, vmem] + [anywhere] * 7 + [vmem] + [anywhere] * 2,
         out_specs=[anywhere, vmem],
         out_shape=[
             jax.ShapeDtypeStruct((1, 2, GRID, HALF), f32),
@@ -358,6 +375,8 @@
             pltpu.VMEM((6, GRID, GRID), bf16),
             pltpu.VMEM((6, GRID, GRID), bf16),
             pltpu.VMEM((GRID, 8 * GRID), bf16),
+            pltpu.VMEM((GRID, GRID), f32),
+            pltpu.SemaphoreType.DMA,
             pltpu.SemaphoreType.DMA,
             pltpu.SemaphoreType.DMA,
             pltpu.SemaphoreType.DMA,
@@ -375,7 +394,7 @@
         partner_behind,
         partner_ahead,
         noise,
-        observed,
+        pltpu.with_memory_space_constraint(observed, pltpu.HBM),
         pltpu.with_memory_space_constraint(jnp.asarray(tables()), pltpu.HBM),
     )
     return moved, misfit.reshape(MOVES, 1)

time: 70 us -> 69.8 us (level)
  local copies, waits for them, and re-layouts: 0.96 us -> 0.02 us
  Pallas kernels: 8.18 us -> 9.04 us
    unnamed x10 -> x6, local copies, waits for them, and re-layouts: 0.96 us -> 0.02 us
    pallas_call x1, Pallas kernels: 0.74 us -> 1.54 us  [body(): pl.pallas_call(functools.partial(first_kernel, lambda: lax.rem(slot_at(),...]
  transfers between devices with their start and end apart: 8 -> 8, of which waited for: 1 -> 1; matrix products, arithmetic and copies ran while one was open for 0% -> 0% of each run, Pallas kernels for 2% -> 3%
where the time goes in v3:
time: 69.8 us; the launch traced here: 69.4 us
  starting transfers between devices  47.3 us (68%)
  waiting for transfers between devices  11.6 us (17%)
  Pallas kernels  9.04 us (13%)
  between operations  1.44 us (2%)
    all_to_all x2, starting transfers between devices, gather(): lax.all_to_all(tiles, 'dom', 0, 0, axis_index_groups=groups, tiled=True)  30.1 us
    ppermute x6, starting transfers between devices, send(): return lax.ppermute(value, 'dom', pairs)  17.3 us
    all_to_all x2, waiting for transfers between devices, gather(): lax.all_to_all(tiles, 'dom', 0, 0, axis_index_groups=groups, tiled=True)  11.5 us
    pallas_call x1, Pallas kernels, body(): pl.pallas_call(functools.partial(final_kernel, slot_at), in_specs=[smem,...  6.83 us
    pallas_call x1, Pallas kernels, body(): pl.pallas_call(functools.partial(first_kernel, lambda: lax.rem(slot_at(),...  1.54 us
  transfers between devices with their start and end apart: 8, of which 1 were waited for; matrix products, arithmetic and copies ran while one was open for 0% of the time, Pallas kernels for 3%

profile of v3, /device:TPU:1, one launch (start us, length us, event | category | flops | bytes accessed | tf_op | source)
XLA Modules:
  0.0 69.4 jit_solution(16304968775797113669)
XLA Ops:
  0.6 1.3 %collective-permute-start.1 = (f32[1,2,256,128]{3,2,1,0:T(8,128)}, f32[1,2,256,128]{3,2,1,0:T(8,128)S(1)}, u32[]{:S(2)}, u32[]{:S(2)}) collective-permute-start(f32[1,2,256,128]{3,2,1,0:T(8,128)} %own_ref.1), channel_id=1, source_target_pairs={{2,0},{3,1},{4,2},{5,3},{6,4},{7,5},{8,6},{9,7},{10,8},{11,9},{12,... | collective-permute-start | bytes 786440 | tf_op jit(solution)/shard_map/ppermute | solution.py:330
  1.9 4.6 %collective-permute-start = (f32[1,2,256,128]{3,2,1,0:T(8,128)}, f32[1,2,256,128]{3,2,1,0:T(8,128)S(1)}, u32[]{:S(2)}, u32[]{:S(2)}) collective-permute-start(f32[1,2,256,128]{3,2,1,0:T(8,128)} %own_ref.1), channel_id=1, source_target_pairs={{0,2},{1,3},{2,4},{3,5},{4,6},{5,7},{6,8},{7,9},{8,10},{9,11},{10,... | collective-permute-start | bytes 786440 | tf_op jit(solution)/shard_map/ppermute | solution.py:330
  7.2 0.0 copy-start
  7.2 0.0 copy-start.1
  7.2 1.5 %first.1 = f32[32,8,128]{2,1,0:T(8,128)} custom-call(f32[8,128]{1,0:T(8,128)S(1)} %broadcast_in_dim.2.offspring_ref, f32[1,2,256,128]{3,2,1,0:T(8,128)} %own_ref.1), custom_call_target="tpu_custom_call" | custom-call | tf_op jit(solution)/shard_map/first/pallas_call | solution.py:333
  8.7 12.3 %all-to-all-start = ((f32[32,8,128]{2,1,0:T(8,128)}), f32[32,8,128]{2,1,0:T(8,128)S(1)}, u32[]{:S(2)}, u32[]{:S(2)}) async-start(f32[32,8,128]{2,1,0:T(8,128)} %first.1), calls=%async_computation | async-start | bytes 262144 | tf_op jit(solution)/shard_map/all_to_all | solution.py:326
  21.1 0.0 copy-done
  21.1 2.1 %collective-permute-start.2 = (f32[1,2,256,128]{3,2,1,0:T(8,128)S(1)}, f32[1,2,256,128]{3,2,1,0:T(8,128)S(1)}, u32[]{:S(2)}, u32[]{:S(2)}) collective-permute-start(f32[1,2,256,128]{3,2,1,0:T(8,128)S(1)} %copy-done), channel_id=1, source_target_pairs={{0,1},{1,0},{2,3},{3,2},{4,5},{5,4},{6,7},{7,6},{8,9},{9,8},{10,11... | collective-permute-start | bytes 786440 | tf_op jit(solution)/shard_map/ppermute | solution.py:330
  23.2 4.9 %collective-permute-start.3 = (f32[1,2,256,128]{3,2,1,0:T(8,128)S(1)}, f32[1,2,256,128]{3,2,1,0:T(8,128)S(1)}, u32[]{:S(2)}, u32[]{:S(2)}) collective-permute-start(f32[1,2,256,128]{3,2,1,0:T(8,128)S(1)} %copy-done), channel_id=1, source_target_pairs={{1,4},{3,6},{4,1},{5,8},{6,3},{7,10},{8,5},{9,12},{10,7},{11,14},{... | collective-permute-start | bytes 786440 | tf_op jit(solution)/shard_map/ppermute | solution.py:330
  28.2 0.0 collective-permute-done.1.ahead_ref
  28.2 1.9 %collective-permute-start.5 = (f32[1,2,256,128]{3,2,1,0:T(8,128)S(1)}, f32[1,2,256,128]{3,2,1,0:T(8,128)S(1)}, u32[]{:S(2)}, u32[]{:S(2)}) collective-permute-start(f32[1,2,256,128]{3,2,1,0:T(8,128)S(1)} %collective-permute-done.1.ahead_ref), channel_id=1, source_target_pairs={{0,1},{1,0},{2,3},{3,2},{4,5},{5,4},{6,7},{7,6},{8,9},{9,8},{10,11... | collective-permute-start | bytes 786440 | tf_op jit(solution)/shard_map/ppermute | solution.py:330
  30.1 0.0 collective-permute-done.behind_ref
  30.1 2.4 %collective-permute-start.4 = (f32[1,2,256,128]{3,2,1,0:T(8,128)S(1)}, f32[1,2,256,128]{3,2,1,0:T(8,128)S(1)}, u32[]{:S(2)}, u32[]{:S(2)}) collective-permute-start(f32[1,2,256,128]{3,2,1,0:T(8,128)S(1)} %collective-permute-done.behind_ref), channel_id=1, source_target_pairs={{0,1},{1,0},{2,3},{3,2},{4,5},{5,4},{6,7},{7,6},{8,9},{9,8},{10,11... | collective-permute-start | bytes 786440 | tf_op jit(solution)/shard_map/ppermute | solution.py:330
  32.5 0.0 all-to-all-done.tiles_ref
  32.6 0.7 second.1
  33.2 17.7 %all-to-all-start.1 = ((f32[16,8,128]{2,1,0:T(8,128)}), f32[16,8,128]{2,1,0:T(8,128)S(1)}, u32[]{:S(2)}, u32[]{:S(2)}) async-start(f32[16,8,128]{2,1,0:T(8,128)} %second.1), calls=%async_computation.1 | async-start | bytes 131072 | tf_op jit(solution)/shard_map/all_to_all | solution.py:326
  51.0 0.0 copy-start.2
  51.0 0.0 collective-permute-done.2.partner_ref
  51.0 0.0 collective-permute-done.3.far_ref
  51.0 11.5 %all-to-all-done.1.tiles_ref = f32[16,8,128]{2,1,0:T(8,128)S(1)} async-done(((f32[16,8,128]{2,1,0:T(8,128)}), f32[16,8,128]{2,1,0:T(8,128)S(1)}, u32[]{:S(2)}, u32[]{:S(2)}) %all-to-all-start.1) | async-done | bytes 65568 | tf_op jit(solution)/shard_map/all_to_all | solution.py:326
  62.5 0.0 collective-permute-done.5.partner_ahead_ref
  62.6 0.0 collective-permute-done.4.partner_behind_ref
  62.6 0.0 copy-done.1
  62.6 0.0 copy-done.2
  62.6 6.8 %final.1 = (f32[1,2,256,128]{3,2,1,0:T(8,128)}, f32[1,2]{1,0:T(1,128)}) custom-call(s32[2]{0:T(128)S(1)} %bitcast.3, f32[16,8,128]{2,1,0:T(8,128)S(1)} %all-to-all-done.1.tiles_ref, f32[1,2,256,128]{3,2,1,0:T(8,128)S(1)} %copy-done, f32[1,2,256,128]{3,2,1,0:T(8,128)S(1)} %collective-permute-done.behind_ref, ...), custom_call_target="tpu_custom_call" | custom-call | tf_op jit(solution)/shard_map/final/pallas_call | solution.py:364
  (1 shorter events, 0.0 us)
Async XLA Ops:
  0.6 27.6 %collective-permute-start.1 = (f32[1,2,256,128]{3,2,1,0:T(8,128)}, f32[1,2,256,128]{3,2,1,0:T(8,128)S(1)}, u32[]{:S(2)}, u32[]{:S(2)}) collective-permute-start(f32[1,2,256,128]{3,2,1,0:T(8,128)} %own_ref.1), channel_id=1, source_target_pairs={{2,0},{3,1},{4,2},{5,3},{6,4},{7,5},{8,6},{9,7},{10,8},{11,9},{12,... | collective-permute-start | bytes 786440 | tf_op jit(solution)/shard_map/ppermute | solution.py:330
  1.9 28.2 %collective-permute-start = (f32[1,2,256,128]{3,2,1,0:T(8,128)}, f32[1,2,256,128]{3,2,1,0:T(8,128)S(1)}, u32[]{:S(2)}, u32[]{:S(2)}) collective-permute-start(f32[1,2,256,128]{3,2,1,0:T(8,128)} %own_ref.1), channel_id=1, source_target_pairs={{0,2},{1,3},{2,4},{3,5},{4,6},{5,7},{6,8},{7,9},{8,10},{9,11},{10,... | collective-permute-start | bytes 786440 | tf_op jit(solution)/shard_map/ppermute | solution.py:330
  7.2 13.9 %copy-start = (f32[1,2,256,128]{3,2,1,0:T(8,128)S(1)}, f32[1,2,256,128]{3,2,1,0:T(8,128)}, u32[]{:S(2)}) copy-start(f32[1,2,256,128]{3,2,1,0:T(8,128)} %own_ref.1) | copy-start | bytes 786436
  7.2 55.4 %copy-start.1 = (f32[2,1,2,256,128]{4,3,2,1,0:T(8,128)S(1)}, f32[2,1,2,256,128]{4,3,2,1,0:T(8,128)}, u32[]{:S(2)}) copy-start(f32[2,1,2,256,128]{4,3,2,1,0:T(8,128)} %noise_ref.1) | copy-start | bytes 1572868
  8.7 23.8 %all-to-all-start = ((f32[32,8,128]{2,1,0:T(8,128)}), f32[32,8,128]{2,1,0:T(8,128)S(1)}, u32[]{:S(2)}, u32[]{:S(2)}) async-start(f32[32,8,128]{2,1,0:T(8,128)} %first.1), calls=%async_computation | async-start | bytes 262144 | tf_op jit(solution)/shard_map/all_to_all | solution.py:326
  21.1 29.9 %collective-permute-start.2 = (f32[1,2,256,128]{3,2,1,0:T(8,128)S(1)}, f32[1,2,256,128]{3,2,1,0:T(8,128)S(1)}, u32[]{:S(2)}, u32[]{:S(2)}) collective-permute-start(f32[1,2,256,128]{3,2,1,0:T(8,128)S(1)} %copy-done), channel_id=1, source_target_pairs={{0,1},{1,0},{2,3},{3,2},{4,5},{5,4},{6,7},{7,6},{8,9},{9,8},{10,11... | collective-permute-start | bytes 786440 | tf_op jit(solution)/shard_map/ppermute | solution.py:330
  23.2 27.8 %collective-permute-start.3 = (f32[1,2,256,128]{3,2,1,0:T(8,128)S(1)}, f32[1,2,256,128]{3,2,1,0:T(8,128)S(1)}, u32[]{:S(2)}, u32[]{:S(2)}) collective-permute-start(f32[1,2,256,128]{3,2,1,0:T(8,128)S(1)} %copy-done), channel_id=1, source_target_pairs={{1,4},{3,6},{4,1},{5,8},{6,3},{7,10},{8,5},{9,12},{10,7},{11,14},{... | collective-permute-start | bytes 786440 | tf_op jit(solution)/shard_map/ppermute | solution.py:330
  28.2 34.4 %collective-permute-start.5 = (f32[1,2,256,128]{3,2,1,0:T(8,128)S(1)}, f32[1,2,256,128]{3,2,1,0:T(8,128)S(1)}, u32[]{:S(2)}, u32[]{:S(2)}) collective-permute-start(f32[1,2,256,128]{3,2,1,0:T(8,128)S(1)} %collective-permute-done.1.ahead_ref), channel_id=1, source_target_pairs={{0,1},{1,0},{2,3},{3,2},{4,5},{5,4},{6,7},{7,6},{8,9},{9,8},{10,11... | collective-permute-start | bytes 786440 | tf_op jit(solution)/shard_map/ppermute | solution.py:330
  30.1 32.4 %collective-permute-start.4 = (f32[1,2,256,128]{3,2,1,0:T(8,128)S(1)}, f32[1,2,256,128]{3,2,1,0:T(8,128)S(1)}, u32[]{:S(2)}, u32[]{:S(2)}) collective-permute-start(f32[1,2,256,128]{3,2,1,0:T(8,128)S(1)} %collective-permute-done.behind_ref), channel_id=1, source_target_pairs={{0,1},{1,0},{2,3},{3,2},{4,5},{5,4},{6,7},{7,6},{8,9},{9,8},{10,11... | collective-permute-start | bytes 786440 | tf_op jit(solution)/shard_map/ppermute | solution.py:330
  33.2 29.3 %all-to-all-start.1 = ((f32[16,8,128]{2,1,0:T(8,128)}), f32[16,8,128]{2,1,0:T(8,128)S(1)}, u32[]{:S(2)}, u32[]{:S(2)}) async-start(f32[16,8,128]{2,1,0:T(8,128)} %second.1), calls=%async_computation.1 | async-start | bytes 131072 | tf_op jit(solution)/shard_map/all_to_all | solution.py:326
  51.0 11.6 %copy-start.2 = (s32[2,1]{0,1:T(1,128)S(1)}, s32[2,1]{0,1:T(1,128)}, u32[]{:S(2)}) copy-start(s32[2,1]{0,1:T(1,128)} %param.9) | copy-start | bytes 28

commit v4 on v3

--- a/solution.py
+++ b/solution.py
@@ -48,6 +48,28 @@
     back = np.concatenate([cos[:, :HALF], sin[:, :HALF]], axis=1)
     parts = [half for t in (across, down, back, across.T) for half in split_table(t)]
     return np.concatenate(parts, axis=1)
+
+
+@functools.lru_cache(maxsize=1)
+def waves():
+    row, wave_x = np.arange(GRID)[:, None], np.arange(HALF)[None, :]
+    wave_y = np.where(row < GRID // 2, row, row - GRID)
+    wave_sq = (wave_y * wave_y + wave_x * wave_x).astype(np.float64)
+    inverse_sq = np.where(wave_sq > 0, 1.0 / np.maximum(wave_sq, 1.0), 0.0)
+    low = (wave_x < LOW) & ((row < LOW // 2) | (row >= GRID - LOW // 2))
+    prior = prior_amplitude / (1.0 + np.sqrt(wave_sq) / 8.0)
+    weight = np.where(wave_x == 0, 1.0, 2.0) / 64.0
+    pull = ((np.abs(wave_y) <= CUT) & (wave_x <= CUT)) * (time_step * 64.0 / (GRID * GRID))
+    return np.stack(
+        [
+            step_size * np.where(low, 1.0, prior),
+            wave_y * inverse_sq,
+            wave_x * inverse_sq,
+            weight / (1.0 + time_step * viscosity * wave_sq),
+            pull * wave_x,
+            pull * wave_y,
+        ]
+    ).astype(np.float32)
 
 
 def lanes(shape):
@@ -77,6 +99,25 @@
     tile_ref[...] = jnp.broadcast_to(tile[None], tile_ref.shape)
 
 
+def pack_kernel(odd_at, own_ref, behind_ref, ahead_ref, pack_ref, pass_ref, sems):
+    copies = [
+        pltpu.make_async_copy(ref.at[0], pack_ref.at[at], sems.at[at])
+        for at, ref in enumerate((own_ref, behind_ref, ahead_ref))
+    ]
+    for copy in copies:
+        copy.start()
+    odd = odd_at()
+    for at, ref in enumerate((ahead_ref, behind_ref)):
+
+        @pl.when(odd == at)
+        def _(ref=ref):
+            pltpu.make_async_copy(ref, pass_ref, sems.at[3]).start()
+
+    pltpu.make_async_copy(behind_ref, pass_ref, sems.at[3]).wait()
+    for copy in copies:
+        copy.wait()
+
+
 def second_kernel(tiles_ref, tile_ref):
     total = tiles_ref[0]
     for at in range(1, PLANE):
@@ -108,35 +149,45 @@
 
 def final_kernel(
     slot_at,
-    accept_ref,
+    accept_hbm,
     tiles_ref,
-    own_ref,
-    behind_ref,
-    ahead_ref,
+    near_ref,
+    far_ref,
     partner_ref,
-    far_ref,
-    partner_behind_ref,
-    partner_ahead_ref,
     noise_ref,
-    observed_ref,
-    table_ref,
+    observed_hbm,
+    waves_hbm,
+    table_hbm,
     moved_ref,
     misfit_ref,
     chosen,
     moved_buf,
     data_high,
     data_low,
+    accept_ref,
+    observed_ref,
+    waves_ref,
     table_buf,
-    observed_buf,
-    table_sem,
-    observed_sem,
+    sems,
     in_sem,
     out_sem,
 ):
-    table_copy = pltpu.make_async_copy(table_ref, table_buf, table_sem)
-    table_copy.start()
-    observed_copy = pltpu.make_async_copy(observed_ref, observed_buf, observed_sem)
-    observed_copy.start()
+    loads = [
+        pltpu.make_async_copy(source, target, sems.at[at])
+        for at, (source, target) in enumerate(
+            (
+                (accept_hbm, accept_ref),
+                (waves_hbm.at[:3], waves_ref.at[:3]),
+                (table_hbm.at[:, : 2 * GRID], table_buf.at[:, : 2 * GRID]),
+                (table_hbm.at[:, 2 * GRID : 4 * GRID], table_buf.at[:, 2 * GRID : 4 * GRID]),
+                (table_hbm.at[:, 4 * GRID :], table_buf.at[:, 4 * GRID :]),
+                (waves_hbm.at[3:], waves_ref.at[3:]),
+                (observed_hbm, observed_ref),
+            )
+        )
+    ]
+    for load in loads:
+        load.start()
     across, down, back, gather = (
         [table_buf.at[:, start : start + GRID] for start in (at, at + GRID)]
         for at in range(0, 8 * GRID, 2 * GRID)
@@ -158,33 +209,25 @@
     offset = jnp.minimum(offset, 3)[0, 0]
 
     side = 1 - 2 * odd
-    candidates = (
-        (0, own_ref),
-        (-2, behind_ref),
-        (2, ahead_ref),
-        (side, partner_ref),
-        (-3 * side, far_ref),
-        (side - 2, partner_behind_ref),
-        (side + 2, partner_ahead_ref),
-    )
-    for at, ref in candidates:
-
-        @pl.when(offset == at)
-        def _(ref=ref):
-            pltpu.make_async_copy(ref.at[0], chosen, in_sem).start()
-
-    row = lax.broadcasted_iota(jnp.int32, (GRID, HALF), 0)
-    wave_x = lanes((GRID, HALF)).astype(f32)
-    wave_y = jnp.where(row < GRID // 2, row, row - GRID).astype(f32)
-    wave_sq = wave_y * wave_y + wave_x * wave_x
-    inverse_sq = jnp.where(wave_sq > 0, 1.0 / jnp.maximum(wave_sq, 1.0), 0.0)
-    along = wave_y * inverse_sq
-    cross = wave_x * inverse_sq
-    weight = jnp.where(lanes((GRID, HALF)) == 0, 1.0 / 64, 2.0 / 64)
-    prior = prior_amplitude / (1.0 + jnp.sqrt(wave_sq) / 8.0)
-    decay = 1.0 / (1.0 + time_step * viscosity * wave_sq)
-    keeper = ((jnp.abs(wave_y) <= CUT) & (wave_x <= CUT)).astype(f32)
-    pull = keeper * (time_step * 64.0 / (GRID * GRID))
+    here = lax.rem(offset + 4, 2) == 0
+    far = offset == -3 * side
+    step = offset - jnp.where(here, 0, side)
+    at = jnp.where(step == 0, 0, jnp.where(step < 0, 1, 2))
+
+    @pl.when(here)
+    def _():
+        pltpu.make_async_copy(near_ref.at[at], chosen, in_sem).start()
+
+    @pl.when(far)
+    def _():
+        pltpu.make_async_copy(far_ref.at[0], chosen, in_sem).start()
+
+    @pl.when(jnp.logical_not(here | far))
+    def _():
+        pltpu.make_async_copy(partner_ref.at[at], chosen, in_sem).start()
+
+    along, cross, damped = (waves_ref.at[i] for i in range(1, 4))
+    weight = jnp.where(lanes((1, HALF)) == 0, 1.0 / 64, 2.0 / 64)
 
     total = tiles_ref[0]
     for at in range(1, RING):
@@ -192,27 +235,29 @@
     adapted = jnp.sqrt(jnp.maximum(total, 0.0) / (RING * PLANE) + 1e-06)
     low_lane = lanes((8, HALF)) < LOW
 
-    def spread(part):
-        top, bottom = adapted, pltpu.roll(adapted, 128 - LOW, 1)
-        if part:
-            top = pltpu.roll(adapted, 128 - 2 * LOW, 1)
-            bottom = pltpu.roll(adapted, 128 - 3 * LOW, 1)
+    factors = [
+        jnp.where(low_lane, pltpu.roll(adapted, (128 - at * LOW) % 128, 1) if at else adapted, 1.0)
+        for at in range(4)
+    ]
+
+    def kick(move, part):
+        value = waves_ref[0] * noise_ref[move, 0, part]
         return jnp.concatenate(
             [
-                jnp.where(low_lane, top, prior[:8]),
-                prior[8 : GRID - 8],
-                jnp.where(low_lane, bottom, prior[GRID - 8 :]),
+                value[:8] * factors[2 * part],
+                value[8 : GRID - 8],
+                value[GRID - 8 :] * factors[2 * part + 1],
             ],
             axis=0,
         )
 
-    scale = [step_size * spread(part) for part in range(2)]
-
-    pltpu.make_async_copy(own_ref.at[0], chosen, in_sem).wait()
+    loads[0].wait()
+    loads[1].wait()
+    pltpu.make_async_copy(far_ref.at[0], chosen, in_sem).wait()
     current = [chosen[part] for part in range(2)]
     proposals = []
     for move in range(MOVES):
-        proposal = [keep * current[part] + scale[part] * noise_ref[move, 0, part] for part in range(2)]
+        proposal = [keep * current[part] + kick(move, part) for part in range(2)]
         proposals.append(proposal)
         taken = accept_ref[move] == 1
         current = [jnp.where(taken, proposal[part], current[part]) for part in range(2)]
@@ -221,8 +266,6 @@
     out_copy = pltpu.make_async_copy(moved_buf, moved_ref.at[0], out_sem)
     out_copy.start()
 
-    table_copy.wait()
-    observed_copy.wait()
 
     def synthesize(at, real, imag):
         for half, value in enumerate((real, imag)):
@@ -274,38 +317,47 @@
         ]
 
     first_row = lax.broadcasted_iota(jnp.int32, (HALF, HALF), 0) == 0
+    loads[2].wait()
+    loads[3].wait()
+    fields = []
+    for move in range(MOVES):
+        wr, wi = (value * weight for value in proposals[move])
+        fields.append(
+            (
+                synthesize(3 * move, wr, wi),
+                synthesize(3 * move + 1, -along[...] * wi, along[...] * wr),
+                synthesize(3 * move + 2, cross[...] * wi, -cross[...] * wr),
+            )
+        )
+    for load in loads[4:]:
+        load.wait()
+    fluxes = [
+        (analyse(6 + 2 * move, flow_u * vort), analyse(7 + 2 * move, flow_v * vort))
+        for move, (vort, flow_u, flow_v) in enumerate(fields)
+    ]
+    finals = []
+    for move, (flux_u, flux_v) in enumerate(fluxes):
+        bands = []
+        for at, start in enumerate((0, GRID - BAND)):
+            kx, ky = (waves_ref[i, start : start + BAND] for i in (4, 5))
+            push = kx * flux_u[at][:, HALF:] + ky * flux_v[at][:, HALF:]
+            lift = kx * flux_u[at][:, :HALF] + ky * flux_v[at][:, :HALF]
+            bands.append((push, lift))
+        middle = jnp.zeros((GRID - 2 * BAND, HALF), f32)
+        change_re, change_im = (
+            jnp.concatenate([bands[0][i], middle, bands[1][i]], axis=0) for i in range(2)
+        )
+        real, imag = proposals[move]
+        finals.append(
+            synthesize(
+                10 + move, (real + change_re) * damped[...], (imag - change_im) * damped[...]
+            )
+        )
     target = jnp.concatenate(
-        [observed_buf[:HALF], backwards(observed_buf[HALF:])], axis=0
-    )
-
+        [observed_ref[:HALF], backwards(observed_ref[HALF:])], axis=0
+    )
     scores = jnp.zeros((1, MOVES), f32)
-    for move in range(MOVES):
-        real, imag = proposals[move]
-        base = 3 * move
-        wr, wi = real * weight, imag * weight
-        vort = synthesize(base, wr, wi)
-        flow_u = synthesize(base + 1, -along * wi, along * wr)
-        flow_v = synthesize(base + 2, cross * wi, -cross * wr)
-        flux_u = analyse(base, flow_u * vort)
-        flux_v = analyse(base + 1, flow_v * vort)
-        push_re, push_im = [], []
-        for at, start in enumerate((0, GRID - BAND)):
-            kx, ky = (w[start : start + BAND] for w in (wave_x, wave_y))
-            factor = pull[start : start + BAND]
-            push_re.append(
-                factor * (kx * flux_u[at][:, HALF:] + ky * flux_v[at][:, HALF:])
-            )
-            push_im.append(
-                -factor * (kx * flux_u[at][:, :HALF] + ky * flux_v[at][:, :HALF])
-            )
-        middle = jnp.zeros((GRID - 2 * BAND, HALF), f32)
-        change_re = jnp.concatenate([push_re[0], middle, push_re[1]], axis=0)
-        change_im = jnp.concatenate([push_im[0], middle, push_im[1]], axis=0)
-        final = synthesize(
-            base + 2,
-            (real + change_re) * decay * weight,
-            (imag + change_im) * decay * weight,
-        )
+    for move, final in enumerate(finals):
         gap = final - target
         score = jnp.sum(gap * gap, keepdims=True) * (
             1.0 / (2.0 * noise_level * noise_level * GRID * GRID)
@@ -329,6 +381,7 @@
         pairs = [(i, target(i)) for i in range(devices) if 0 <= target(i) < devices]
         return lax.ppermute(value, "dom", pairs)
 
+    in_hbm = functools.partial(pltpu.with_memory_space_constraint, memory_space=pltpu.HBM)
     slot_at = lambda: lax.axis_index("dom")
     tile = pl.pallas_call(
         functools.partial(first_kernel, lambda: lax.rem(slot_at(), PLANE)),
@@ -347,8 +400,6 @@
     )
     behind = send(particles, lambda i: i + 2)
     ahead = send(particles, lambda i: i - 2)
-    partner = send(particles, lambda i: i ^ 1)
-    far = send(particles, lambda i: i + 3 if i % 2 else i - 3)
     plane = gather(tile, planes)
     tile = pl.pallas_call(
         second_kernel,
@@ -358,12 +409,24 @@
         compiler_params=pltpu.CompilerParams(vmem_limit_bytes=2 * 1024 * 1024),
         name="second",
     )(plane)
-    partner_behind = send(behind, lambda i: i ^ 1)
-    partner_ahead = send(ahead, lambda i: i ^ 1)
+    packed, passed = pl.pallas_call(
+        functools.partial(pack_kernel, lambda: lax.rem(slot_at(), 2)),
+        in_specs=[anywhere] * 3,
+        out_specs=[anywhere] * 2,
+        out_shape=[
+            jax.ShapeDtypeStruct((3, 2, GRID, HALF), f32),
+            jax.ShapeDtypeStruct((1, 2, GRID, HALF), f32),
+        ],
+        scratch_shapes=[pltpu.SemaphoreType.DMA((4,))],
+        compiler_params=pltpu.CompilerParams(vmem_limit_bytes=2 * 1024 * 1024),
+        name="pack",
+    )(particles, behind, ahead)
+    far = send(passed, lambda i: i + 1 if i % 2 else i - 1)
+    partner = send(packed, lambda i: i ^ 1)
     tiles = gather(tile, rings)
     moved, misfit = pl.pallas_call(
         functools.partial(final_kernel, slot_at),
-        in_specs=[smem, vmem] + [anywhere] * 7 + [vmem] + [anywhere] * 2,
+        in_specs=[anywhere, vmem] + [anywhere] * 3 + [vmem] + [anywhere] * 3,
         out_specs=[anywhere, vmem],
         out_shape=[
             jax.ShapeDtypeStruct((1, 2, GRID, HALF), f32),
@@ -372,30 +435,28 @@
         scratch_shapes=[
             pltpu.VMEM((2, GRID, HALF), f32),
             pltpu.VMEM((2, GRID, HALF), f32),
-            pltpu.VMEM((6, GRID, GRID), bf16),
-            pltpu.VMEM((6, GRID, GRID), bf16),
+            pltpu.VMEM((12, GRID, GRID), bf16),
+            pltpu.VMEM((12, GRID, GRID), bf16),
+            pltpu.SMEM((MOVES,), jnp.int32),
+            pltpu.VMEM((GRID, GRID), f32),
+            pltpu.VMEM((6, GRID, HALF), f32),
             pltpu.VMEM((GRID, 8 * GRID), bf16),
-            pltpu.VMEM((GRID, GRID), f32),
-            pltpu.SemaphoreType.DMA,
-            pltpu.SemaphoreType.DMA,
+            pltpu.SemaphoreType.DMA((7,)),
             pltpu.SemaphoreType.DMA,
             pltpu.SemaphoreType.DMA,
         ],
         compiler_params=pltpu.CompilerParams(vmem_limit_bytes=24 * 1024 * 1024),
         name="final",
     )(
-        accept.reshape(MOVES),
+        in_hbm(accept.reshape(MOVES)),
         tiles,
-        particles,
-        behind,
-        ahead,
+        packed,
+        far,
         partner,
-        far,
-        partner_behind,
-        partner_ahead,
         noise,
-        pltpu.with_memory_space_constraint(observed, pltpu.HBM),
-        pltpu.with_memory_space_constraint(jnp.asarray(tables()), pltpu.HBM),
+        in_hbm(observed),
+        in_hbm(jnp.asarray(waves())),
+        in_hbm(jnp.asarray(tables())),
     )
     return moved, misfit.reshape(MOVES, 1)
 

time: 69.8 us -> 72 us (1.032)
  blocking collectives: 0 us -> 26.1 us
  starting transfers between devices: 47.3 us -> 25.3 us
  Pallas kernels: 9.04 us -> 7.31 us
  waiting for transfers between devices: 11.6 us -> 10.1 us
  local copies, waits for them, and re-layouts: 0.02 us -> 0.96 us
    all_to_all x0 -> x1, blocking collectives: none -> 26.1 us  [gather(): lax.all_to_all(tiles, 'dom', 0, 0, axis_index_groups=groups, tiled=True)]
    all_to_all x2 -> x1, starting transfers between devices: 30.1 us -> 9.13 us  [gather(): lax.all_to_all(tiles, 'dom', 0, 0, axis_index_groups=groups, tiled=True)]
    all_to_all x2 -> x1, waiting for transfers between devices: 11.5 us -> 4.05 us  [gather(): lax.all_to_all(tiles, 'dom', 0, 0, axis_index_groups=groups, tiled=True)]
    ppermute x6 -> x4, waiting for transfers between devices: 0.02 us -> 6.03 us  [send(): return lax.ppermute(value, 'dom', pairs)]
    ppermute x6 -> x4, starting transfers between devices: 17.3 us -> 16.2 us  [send(): return lax.ppermute(value, 'dom', pairs)]
    pallas_call x1 -> x2, Pallas kernels: 6.83 us -> 5.8 us  [the longest x1 5.67 us: body(): pl.pallas_call(functools.partial(final_kernel, slot_at), in_specs=[anywhe...]
    unnamed x6 -> x4, local copies, waits for them, and re-layouts: 0.02 us -> 0.96 us
  transfers between devices with their start and end apart: 8 -> 5, of which waited for: 1 -> 3; matrix products, arithmetic and copies ran while one was open for 0% -> 0% of each run, Pallas kernels for 3% -> 2%
where the time goes in v4:
time: 72 us; the launch traced here: 71.1 us
  blocking collectives  26.1 us (36%)
  starting transfers between devices  25.3 us (35%)
  waiting for transfers between devices  10.1 us (14%)
  Pallas kernels  7.31 us (10%)
  between operations  1.36 us (2%)
  local copies, waits for them, and re-layouts  0.96 us (1%)
    all_to_all x1, blocking collectives, gather(): lax.all_to_all(tiles, 'dom', 0, 0, axis_index_groups=groups, tiled=True)  26.1 us
    ppermute x4, starting transfers between devices, send(): return lax.ppermute(value, 'dom', pairs)  16.2 us
    all_to_all x1, starting transfers between devices, gather(): lax.all_to_all(tiles, 'dom', 0, 0, axis_index_groups=groups, tiled=True)  9.13 us
    ppermute x4, waiting for transfers between devices, send(): return lax.ppermute(value, 'dom', pairs)  6.03 us
    pallas_call x1, Pallas kernels, body(): pl.pallas_call(functools.partial(final_kernel, slot_at), in_specs=[anywhe...  5.67 us
    all_to_all x1, waiting for transfers between devices, gather(): lax.all_to_all(tiles, 'dom', 0, 0, axis_index_groups=groups, tiled=True)  4.05 us
    pallas_call x1, Pallas kernels, body(): pl.pallas_call(functools.partial(first_kernel, lambda: lax.rem(slot_at(),...  1.47 us
  transfers between devices with their start and end apart: 5, of which 3 were waited for; matrix products, arithmetic and copies ran while one was open for 0% of the time, Pallas kernels for 2%

profile of v4, /device:TPU:1, one launch (start us, length us, event | category | flops | bytes accessed | tf_op | source)
XLA Modules:
  0.0 71.1 jit_solution(17958331455586474625)
XLA Ops:
  0.6 4.0 %collective-permute-start = (f32[1,2,256,128]{3,2,1,0:T(8,128)}, f32[1,2,256,128]{3,2,1,0:T(8,128)S(1)}, u32[]{:S(2)}, u32[]{:S(2)}) collective-permute-start(f32[1,2,256,128]{3,2,1,0:T(8,128)} %own_ref.1), channel_id=1, source_target_pairs={{0,2},{1,3},{2,4},{3,5},{4,6},{5,7},{6,8},{7,9},{8,10},{9,11},{10,... | collective-permute-start | bytes 786440 | tf_op jit(solution)/shard_map/ppermute | solution.py:382
  4.6 1.3 %collective-permute-start.1 = (f32[1,2,256,128]{3,2,1,0:T(8,128)}, f32[1,2,256,128]{3,2,1,0:T(8,128)S(1)}, u32[]{:S(2)}, u32[]{:S(2)}) collective-permute-start(f32[1,2,256,128]{3,2,1,0:T(8,128)} %own_ref.1), channel_id=1, source_target_pairs={{2,0},{3,1},{4,2},{5,3},{6,4},{7,5},{8,6},{9,7},{10,8},{11,9},{12,... | collective-permute-start | bytes 786440 | tf_op jit(solution)/shard_map/ppermute | solution.py:382
  5.9 2.3 %collective-permute-done.behind_ref = f32[1,2,256,128]{3,2,1,0:T(8,128)S(1)} collective-permute-done((f32[1,2,256,128]{3,2,1,0:T(8,128)}, f32[1,2,256,128]{3,2,1,0:T(8,128)S(1)}, u32[]{:S(2)}, u32[]{:S(2)}) %collective-permute-start) | collective-permute-done | bytes 262176 | tf_op jit(solution)/shard_map/ppermute | solution.py:382
  8.2 3.7 %collective-permute-done.1.ahead_ref = f32[1,2,256,128]{3,2,1,0:T(8,128)S(1)} collective-permute-done((f32[1,2,256,128]{3,2,1,0:T(8,128)}, f32[1,2,256,128]{3,2,1,0:T(8,128)S(1)}, u32[]{:S(2)}, u32[]{:S(2)}) %collective-permute-start.1) | collective-permute-done | bytes 262176 | tf_op jit(solution)/shard_map/ppermute | solution.py:382
  11.9 0.0 copy-start
  11.9 0.9 %copy-done = f32[1,2,256,128]{3,2,1,0:T(8,128)S(1)} copy-done((f32[1,2,256,128]{3,2,1,0:T(8,128)S(1)}, f32[1,2,256,128]{3,2,1,0:T(8,128)}, u32[]{:S(2)}) %copy-start) | copy-done | bytes 262168
  12.9 0.1 pack.1
  13.0 0.0 copy-start.1
  13.0 7.4 %collective-permute-start.3 = (f32[3,2,256,128]{3,2,1,0:T(8,128)S(1)}, f32[3,2,256,128]{3,2,1,0:T(8,128)S(1)}, u32[]{:S(2)}, u32[]{:S(2)}) collective-permute-start(f32[3,2,256,128]{3,2,1,0:T(8,128)S(1)} %get-tuple-element.6.near_ref), channel_id=1, source_target_pairs={{0,1},{1,0},{2,3},{3,2},{4,5},{5,4},{6,7},{7,6},{8,9},{9,8},{10,11... | collective-permute-start | bytes 2359304 | tf_op jit(solution)/shard_map/ppermute | solution.py:382
  21.1 1.5 %first.1 = f32[32,8,128]{2,1,0:T(8,128)} custom-call(f32[8,128]{1,0:T(8,128)S(1)} %broadcast_in_dim.2.offspring_ref, f32[1,2,256,128]{3,2,1,0:T(8,128)} %own_ref.1), custom_call_target="tpu_custom_call" | custom-call | tf_op jit(solution)/shard_map/first/pallas_call | solution.py:386
  22.5 9.1 %all-to-all-start = ((f32[32,8,128]{2,1,0:T(8,128)}), f32[32,8,128]{2,1,0:T(8,128)S(1)}, u32[]{:S(2)}, u32[]{:S(2)}) async-start(f32[32,8,128]{2,1,0:T(8,128)} %first.1), calls=%async_computation | async-start | bytes 262144 | tf_op jit(solution)/shard_map/all_to_all | solution.py:378
  31.7 3.5 %collective-permute-start.2 = (f32[1,2,256,128]{3,2,1,0:T(8,128)S(1)}, f32[1,2,256,128]{3,2,1,0:T(8,128)S(1)}, u32[]{:S(2)}, u32[]{:S(2)}) collective-permute-start(f32[1,2,256,128]{3,2,1,0:T(8,128)S(1)} %get-tuple-element.7), channel_id=1, source_target_pairs={{1,2},{2,1},{3,4},{4,3},{5,6},{6,5},{7,8},{8,7},{9,10},{10,9},{11,... | collective-permute-start | bytes 786440 | tf_op jit(solution)/shard_map/ppermute | solution.py:382
  35.2 4.1 %all-to-all-done.tiles_ref = f32[32,8,128]{2,1,0:T(8,128)S(1)} async-done(((f32[32,8,128]{2,1,0:T(8,128)}), f32[32,8,128]{2,1,0:T(8,128)S(1)}, u32[]{:S(2)}, u32[]{:S(2)}) %all-to-all-start) | async-done | bytes 131104 | tf_op jit(solution)/shard_map/all_to_all | solution.py:378
  39.3 26.1 %all_to_all.10.tiles_ref = f32[16,8,128]{2,1,0:T(8,128)S(1)} all-to-all(f32[16,8,128]{2,1,0:T(8,128)S(1)} %second.1), channel_id=1, replica_groups={{0,32,64,96,128,160,192,224,256,288,320,352,384,416,448,480},{1,33,65,9..., dimensions={0} | all-to-all | bytes 131072 | tf_op jit(solution)/shard_map/all_to_all | solution.py:378
  65.5 0.0 collective-permute-done.2.far_ref
  65.5 0.0 collective-permute-done.3.partner_ref
  65.5 0.0 copy-done.1
  65.5 5.7 %final.1 = (f32[1,2,256,128]{3,2,1,0:T(8,128)}, f32[1,2]{1,0:T(1,128)}) custom-call(s32[2]{0:T(128)} %bitcast.3, f32[16,8,128]{2,1,0:T(8,128)S(1)} %all_to_all.10.tiles_ref, f32[3,2,256,128]{3,2,1,0:T(8,128)S(1)} %get-tuple-element.6.near_ref, f32[1,2,256,128]{3,2,1,0:T(8,128)S(1)} %collective-permute-done.2.far_ref, ...), custom_call_target="tpu_custom_call" | custom-call | tf_op jit(solution)/shard_map/final/pallas_call | solution.py:427
  (2 shorter events, 0.0 us)
Async XLA Ops:
  0.6 7.6 %collective-permute-start = (f32[1,2,256,128]{3,2,1,0:T(8,128)}, f32[1,2,256,128]{3,2,1,0:T(8,128)S(1)}, u32[]{:S(2)}, u32[]{:S(2)}) collective-permute-start(f32[1,2,256,128]{3,2,1,0:T(8,128)} %own_ref.1), channel_id=1, source_target_pairs={{0,2},{1,3},{2,4},{3,5},{4,6},{5,7},{6,8},{7,9},{8,10},{9,11},{10,... | collective-permute-start | bytes 786440 | tf_op jit(solution)/shard_map/ppermute | solution.py:382
  4.6 7.3 %collective-permute-start.1 = (f32[1,2,256,128]{3,2,1,0:T(8,128)}, f32[1,2,256,128]{3,2,1,0:T(8,128)S(1)}, u32[]{:S(2)}, u32[]{:S(2)}) collective-permute-start(f32[1,2,256,128]{3,2,1,0:T(8,128)} %own_ref.1), channel_id=1, source_target_pairs={{2,0},{3,1},{4,2},{5,3},{6,4},{7,5},{8,6},{9,7},{10,8},{11,9},{12,... | collective-permute-start | bytes 786440 | tf_op jit(solution)/shard_map/ppermute | solution.py:382
  11.9 1.0 %copy-start = (f32[1,2,256,128]{3,2,1,0:T(8,128)S(1)}, f32[1,2,256,128]{3,2,1,0:T(8,128)}, u32[]{:S(2)}) copy-start(f32[1,2,256,128]{3,2,1,0:T(8,128)} %own_ref.1) | copy-start | bytes 786436
  13.0 52.5 %copy-start.1 = (f32[2,1,2,256,128]{4,3,2,1,0:T(8,128)S(1)}, f32[2,1,2,256,128]{4,3,2,1,0:T(8,128)}, u32[]{:S(2)}) copy-start(f32[2,1,2,256,128]{4,3,2,1,0:T(8,128)} %noise_ref.1) | copy-start | bytes 1572868
  13.0 52.5 %collective-permute-start.3 = (f32[3,2,256,128]{3,2,1,0:T(8,128)S(1)}, f32[3,2,256,128]{3,2,1,0:T(8,128)S(1)}, u32[]{:S(2)}, u32[]{:S(2)}) collective-permute-start(f32[3,2,256,128]{3,2,1,0:T(8,128)S(1)} %get-tuple-element.6.near_ref), channel_id=1, source_target_pairs={{0,1},{1,0},{2,3},{3,2},{4,5},{5,4},{6,7},{7,6},{8,9},{9,8},{10,11... | collective-permute-start | bytes 2359304 | tf_op jit(solution)/shard_map/ppermute | solution.py:382
  22.5 16.7 %all-to-all-start = ((f32[32,8,128]{2,1,0:T(8,128)}), f32[32,8,128]{2,1,0:T(8,128)S(1)}, u32[]{:S(2)}, u32[]{:S(2)}) async-start(f32[32,8,128]{2,1,0:T(8,128)} %first.1), calls=%async_computation | async-start | bytes 262144 | tf_op jit(solution)/shard_map/all_to_all | solution.py:378
  31.7 33.8 %collective-permute-start.2 = (f32[1,2,256,128]{3,2,1,0:T(8,128)S(1)}, f32[1,2,256,128]{3,2,1,0:T(8,128)S(1)}, u32[]{:S(2)}, u32[]{:S(2)}) collective-permute-start(f32[1,2,256,128]{3,2,1,0:T(8,128)S(1)} %get-tuple-element.7), channel_id=1, source_target_pairs={{1,2},{2,1},{3,4},{4,3},{5,6},{6,5},{7,8},{8,7},{9,10},{10,9},{11,... | collective-permute-start | bytes 786440 | tf_op jit(solution)/shard_map/ppermute | solution.py:382

commit v5 on v4

--- a/solution.py
+++ b/solution.py
@@ -99,21 +99,13 @@
     tile_ref[...] = jnp.broadcast_to(tile[None], tile_ref.shape)
 
 
-def pack_kernel(odd_at, own_ref, behind_ref, ahead_ref, pack_ref, pass_ref, sems):
+def pack_kernel(own_ref, behind_ref, ahead_ref, pack_ref, sems):
     copies = [
         pltpu.make_async_copy(ref.at[0], pack_ref.at[at], sems.at[at])
         for at, ref in enumerate((own_ref, behind_ref, ahead_ref))
     ]
     for copy in copies:
         copy.start()
-    odd = odd_at()
-    for at, ref in enumerate((ahead_ref, behind_ref)):
-
-        @pl.when(odd == at)
-        def _(ref=ref):
-            pltpu.make_async_copy(ref, pass_ref, sems.at[3]).start()
-
-    pltpu.make_async_copy(behind_ref, pass_ref, sems.at[3]).wait()
     for copy in copies:
         copy.wait()
 
@@ -409,19 +401,16 @@
         compiler_params=pltpu.CompilerParams(vmem_limit_bytes=2 * 1024 * 1024),
         name="second",
     )(plane)
-    packed, passed = pl.pallas_call(
-        functools.partial(pack_kernel, lambda: lax.rem(slot_at(), 2)),
+    packed = pl.pallas_call(
+        pack_kernel,
         in_specs=[anywhere] * 3,
-        out_specs=[anywhere] * 2,
-        out_shape=[
-            jax.ShapeDtypeStruct((3, 2, GRID, HALF), f32),
-            jax.ShapeDtypeStruct((1, 2, GRID, HALF), f32),
-        ],
-        scratch_shapes=[pltpu.SemaphoreType.DMA((4,))],
+        out_specs=anywhere,
+        out_shape=jax.ShapeDtypeStruct((3, 2, GRID, HALF), f32),
+        scratch_shapes=[pltpu.SemaphoreType.DMA((3,))],
         compiler_params=pltpu.CompilerParams(vmem_limit_bytes=2 * 1024 * 1024),
         name="pack",
     )(particles, behind, ahead)
-    far = send(passed, lambda i: i + 1 if i % 2 else i - 1)
+    far = send(particles, lambda i: i + 3 if i % 2 else i - 3)
     partner = send(packed, lambda i: i ^ 1)
     tiles = gather(tile, rings)
     moved, misfit = pl.pallas_call(

time: 72 us -> 73.9 us (1.026)
  blocking collectives: 26.1 us -> 0 us
  starting transfers between devices: 25.3 us -> 45.5 us
  waiting for transfers between devices: 10.1 us -> 17.7 us
    all_to_all x1 -> x0, blocking collectives: 26.1 us -> none  [gather(): lax.all_to_all(tiles, 'dom', 0, 0, axis_index_groups=groups, tiled=True)]
    all_to_all x1 -> x2, starting transfers between devices: 9.13 us -> 25.1 us  [gather(): lax.all_to_all(tiles, 'dom', 0, 0, axis_index_groups=groups, tiled=True)]
    all_to_all x1 -> x2, waiting for transfers between devices: 4.05 us -> 14.1 us  [gather(): lax.all_to_all(tiles, 'dom', 0, 0, axis_index_groups=groups, tiled=True)]
    ppermute x4, starting transfers between devices: 16.2 us -> 20.4 us  [send(): return lax.ppermute(value, 'dom', pairs)]
    ppermute x4, waiting for transfers between devices: 6.03 us -> 3.6 us  [send(): return lax.ppermute(value, 'dom', pairs)]
  transfers between devices with their start and end apart: 5 -> 6, of which waited for: 3 -> 4; matrix products, arithmetic and copies ran while one was open for 0% -> 0% of each run, Pallas kernels for 2% -> 3%
where the time goes in v5:
time: 73.9 us; the launch traced here: 73.5 us
  starting transfers between devices  45.5 us (62%)
  waiting for transfers between devices  17.7 us (24%)
  Pallas kernels  7.94 us (11%)
  between operations  1.38 us (2%)
  local copies, waits for them, and re-layouts  0.96 us (1%)
    all_to_all x2, starting transfers between devices, gather(): lax.all_to_all(tiles, 'dom', 0, 0, axis_index_groups=groups, tiled=True)  25.1 us
    ppermute x4, starting transfers between devices, send(): return lax.ppermute(value, 'dom', pairs)  20.4 us
    all_to_all x2, waiting for transfers between devices, gather(): lax.all_to_all(tiles, 'dom', 0, 0, axis_index_groups=groups, tiled=True)  14.1 us
    pallas_call x1, Pallas kernels, body(): pl.pallas_call(functools.partial(final_kernel, slot_at), in_specs=[anywhe...  5.67 us
    ppermute x4, waiting for transfers between devices, send(): return lax.ppermute(value, 'dom', pairs)  3.6 us
    pallas_call x1, Pallas kernels, body(): pl.pallas_call(functools.partial(first_kernel, lambda: lax.rem(slot_at(),...  1.52 us
  transfers between devices with their start and end apart: 6, of which 4 were waited for; matrix products, arithmetic and copies ran while one was open for 0% of the time, Pallas kernels for 3%

profile of v5, /device:TPU:1, one launch (start us, length us, event | category | flops | bytes accessed | tf_op | source)
XLA Modules:
  0.0 73.5 jit_solution(1533127453517233900)
XLA Ops:
  0.6 1.3 %collective-permute-start.1 = (f32[1,2,256,128]{3,2,1,0:T(8,128)}, f32[1,2,256,128]{3,2,1,0:T(8,128)S(1)}, u32[]{:S(2)}, u32[]{:S(2)}) collective-permute-start(f32[1,2,256,128]{3,2,1,0:T(8,128)} %own_ref.1), channel_id=1, source_target_pairs={{2,0},{3,1},{4,2},{5,3},{6,4},{7,5},{8,6},{9,7},{10,8},{11,9},{12,... | collective-permute-start | bytes 786440 | tf_op jit(solution)/shard_map/ppermute | solution.py:374
  1.9 4.6 %collective-permute-start = (f32[1,2,256,128]{3,2,1,0:T(8,128)}, f32[1,2,256,128]{3,2,1,0:T(8,128)S(1)}, u32[]{:S(2)}, u32[]{:S(2)}) collective-permute-start(f32[1,2,256,128]{3,2,1,0:T(8,128)} %own_ref.1), channel_id=1, source_target_pairs={{0,2},{1,3},{2,4},{3,5},{4,6},{5,7},{6,8},{7,9},{8,10},{9,11},{10,... | collective-permute-start | bytes 786440 | tf_op jit(solution)/shard_map/ppermute | solution.py:374
  6.5 2.0 %collective-permute-done.1.ahead_ref = f32[1,2,256,128]{3,2,1,0:T(8,128)S(1)} collective-permute-done((f32[1,2,256,128]{3,2,1,0:T(8,128)}, f32[1,2,256,128]{3,2,1,0:T(8,128)S(1)}, u32[]{:S(2)}, u32[]{:S(2)}) %collective-permute-start.1) | collective-permute-done | bytes 262176 | tf_op jit(solution)/shard_map/ppermute | solution.py:374
  8.5 1.6 %collective-permute-done.behind_ref = f32[1,2,256,128]{3,2,1,0:T(8,128)S(1)} collective-permute-done((f32[1,2,256,128]{3,2,1,0:T(8,128)}, f32[1,2,256,128]{3,2,1,0:T(8,128)S(1)}, u32[]{:S(2)}, u32[]{:S(2)}) %collective-permute-start) | collective-permute-done | bytes 262176 | tf_op jit(solution)/shard_map/ppermute | solution.py:374
  10.1 0.0 copy-start
  10.1 0.9 %copy-done = f32[1,2,256,128]{3,2,1,0:T(8,128)S(1)} copy-done((f32[1,2,256,128]{3,2,1,0:T(8,128)S(1)}, f32[1,2,256,128]{3,2,1,0:T(8,128)}, u32[]{:S(2)}) %copy-start) | copy-done | bytes 262168
  11.1 0.0 copy-start.2
  11.1 0.1 pack.1.near_ref
  11.2 9.4 %collective-permute-start.3 = (f32[3,2,256,128]{3,2,1,0:T(8,128)S(1)}, f32[3,2,256,128]{3,2,1,0:T(8,128)S(1)}, u32[]{:S(2)}, u32[]{:S(2)}) collective-permute-start(f32[3,2,256,128]{3,2,1,0:T(8,128)S(1)} %pack.1.near_ref), channel_id=1, source_target_pairs={{0,1},{1,0},{2,3},{3,2},{4,5},{5,4},{6,7},{7,6},{8,9},{9,8},{10,11... | collective-permute-start | bytes 2359304 | tf_op jit(solution)/shard_map/ppermute | solution.py:374
  21.3 0.0 copy-start.1
  21.3 1.5 %first.1 = f32[32,8,128]{2,1,0:T(8,128)} custom-call(f32[8,128]{1,0:T(8,128)S(1)} %broadcast_in_dim.2.offspring_ref, f32[1,2,256,128]{3,2,1,0:T(8,128)} %own_ref.1), custom_call_target="tpu_custom_call" | custom-call | tf_op jit(solution)/shard_map/first/pallas_call | solution.py:378
  22.8 7.0 %all-to-all-start = ((f32[32,8,128]{2,1,0:T(8,128)}), f32[32,8,128]{2,1,0:T(8,128)S(1)}, u32[]{:S(2)}, u32[]{:S(2)}) async-start(f32[32,8,128]{2,1,0:T(8,128)} %first.1), calls=%async_computation | async-start | bytes 262144 | tf_op jit(solution)/shard_map/all_to_all | solution.py:370
  29.8 0.0 copy-done.1
  29.9 5.0 %collective-permute-start.2 = (f32[1,2,256,128]{3,2,1,0:T(8,128)S(1)}, f32[1,2,256,128]{3,2,1,0:T(8,128)S(1)}, u32[]{:S(2)}, u32[]{:S(2)}) collective-permute-start(f32[1,2,256,128]{3,2,1,0:T(8,128)S(1)} %copy-done.1), channel_id=1, source_target_pairs={{1,4},{3,6},{4,1},{5,8},{6,3},{7,10},{8,5},{9,12},{10,7},{11,14},{... | collective-permute-start | bytes 786440 | tf_op jit(solution)/shard_map/ppermute | solution.py:374
  34.9 2.5 %all-to-all-done.tiles_ref = f32[32,8,128]{2,1,0:T(8,128)S(1)} async-done(((f32[32,8,128]{2,1,0:T(8,128)}), f32[32,8,128]{2,1,0:T(8,128)S(1)}, u32[]{:S(2)}, u32[]{:S(2)}) %all-to-all-start) | async-done | bytes 131104 | tf_op jit(solution)/shard_map/all_to_all | solution.py:370
  37.4 0.7 second.1
  38.1 18.1 %all-to-all-start.1 = ((f32[16,8,128]{2,1,0:T(8,128)}), f32[16,8,128]{2,1,0:T(8,128)S(1)}, u32[]{:S(2)}, u32[]{:S(2)}) async-start(f32[16,8,128]{2,1,0:T(8,128)} %second.1), calls=%async_computation.1 | async-start | bytes 131072 | tf_op jit(solution)/shard_map/all_to_all | solution.py:370
  56.2 0.0 collective-permute-done.2.far_ref
  56.2 11.6 %all-to-all-done.1.tiles_ref = f32[16,8,128]{2,1,0:T(8,128)S(1)} async-done(((f32[16,8,128]{2,1,0:T(8,128)}), f32[16,8,128]{2,1,0:T(8,128)S(1)}, u32[]{:S(2)}, u32[]{:S(2)}) %all-to-all-start.1) | async-done | bytes 65568 | tf_op jit(solution)/shard_map/all_to_all | solution.py:370
  67.8 0.0 collective-permute-done.3.partner_ref
  67.8 0.0 copy-done.2
  67.8 5.7 %final.1 = (f32[1,2,256,128]{3,2,1,0:T(8,128)}, f32[1,2]{1,0:T(1,128)}) custom-call(s32[2]{0:T(128)} %bitcast.3, f32[16,8,128]{2,1,0:T(8,128)S(1)} %all-to-all-done.1.tiles_ref, f32[3,2,256,128]{3,2,1,0:T(8,128)S(1)} %pack.1.near_ref, f32[1,2,256,128]{3,2,1,0:T(8,128)S(1)} %collective-permute-done.2.far_ref, ...), custom_call_target="tpu_custom_call" | custom-call | tf_op jit(solution)/shard_map/final/pallas_call | solution.py:416
  (1 shorter events, 0.0 us)
Async XLA Ops:
  0.6 7.9 %collective-permute-start.1 = (f32[1,2,256,128]{3,2,1,0:T(8,128)}, f32[1,2,256,128]{3,2,1,0:T(8,128)S(1)}, u32[]{:S(2)}, u32[]{:S(2)}) collective-permute-start(f32[1,2,256,128]{3,2,1,0:T(8,128)} %own_ref.1), channel_id=1, source_target_pairs={{2,0},{3,1},{4,2},{5,3},{6,4},{7,5},{8,6},{9,7},{10,8},{11,9},{12,... | collective-permute-start | bytes 786440 | tf_op jit(solution)/shard_map/ppermute | solution.py:374
  1.9 8.2 %collective-permute-start = (f32[1,2,256,128]{3,2,1,0:T(8,128)}, f32[1,2,256,128]{3,2,1,0:T(8,128)S(1)}, u32[]{:S(2)}, u32[]{:S(2)}) collective-permute-start(f32[1,2,256,128]{3,2,1,0:T(8,128)} %own_ref.1), channel_id=1, source_target_pairs={{0,2},{1,3},{2,4},{3,5},{4,6},{5,7},{6,8},{7,9},{8,10},{9,11},{10,... | collective-permute-start | bytes 786440 | tf_op jit(solution)/shard_map/ppermute | solution.py:374
  10.1 0.9 %copy-start = (f32[1,2,256,128]{3,2,1,0:T(8,128)S(1)}, f32[1,2,256,128]{3,2,1,0:T(8,128)}, u32[]{:S(2)}) copy-start(f32[1,2,256,128]{3,2,1,0:T(8,128)} %own_ref.1) | copy-start | bytes 786436
  11.1 56.8 %copy-start.2 = (f32[2,1,2,256,128]{4,3,2,1,0:T(8,128)S(1)}, f32[2,1,2,256,128]{4,3,2,1,0:T(8,128)}, u32[]{:S(2)}) copy-start(f32[2,1,2,256,128]{4,3,2,1,0:T(8,128)} %noise_ref.1) | copy-start | bytes 1572868
  11.2 56.7 %collective-permute-start.3 = (f32[3,2,256,128]{3,2,1,0:T(8,128)S(1)}, f32[3,2,256,128]{3,2,1,0:T(8,128)S(1)}, u32[]{:S(2)}, u32[]{:S(2)}) collective-permute-start(f32[3,2,256,128]{3,2,1,0:T(8,128)S(1)} %pack.1.near_ref), channel_id=1, source_target_pairs={{0,1},{1,0},{2,3},{3,2},{4,5},{5,4},{6,7},{7,6},{8,9},{9,8},{10,11... | collective-permute-start | bytes 2359304 | tf_op jit(solution)/shard_map/ppermute | solution.py:374
  21.3 8.6 %copy-start.1 = (f32[1,2,256,128]{3,2,1,0:T(8,128)S(1)}, f32[1,2,256,128]{3,2,1,0:T(8,128)}, u32[]{:S(2)}) copy-start(f32[1,2,256,128]{3,2,1,0:T(8,128)} %own_ref.1) | copy-start | bytes 786436
  22.8 14.6 %all-to-all-start = ((f32[32,8,128]{2,1,0:T(8,128)}), f32[32,8,128]{2,1,0:T(8,128)S(1)}, u32[]{:S(2)}, u32[]{:S(2)}) async-start(f32[32,8,128]{2,1,0:T(8,128)} %first.1), calls=%async_computation | async-start | bytes 262144 | tf_op jit(solution)/shard_map/all_to_all | solution.py:370
  29.9 26.4 %collective-permute-start.2 = (f32[1,2,256,128]{3,2,1,0:T(8,128)S(1)}, f32[1,2,256,128]{3,2,1,0:T(8,128)S(1)}, u32[]{:S(2)}, u32[]{:S(2)}) collective-permute-start(f32[1,2,256,128]{3,2,1,0:T(8,128)S(1)} %copy-done.1), channel_id=1, source_target_pairs={{1,4},{3,6},{4,1},{5,8},{6,3},{7,10},{8,5},{9,12},{10,7},{11,14},{... | collective-permute-start | bytes 786440 | tf_op jit(solution)/shard_map/ppermute | solution.py:374
  38.1 29.7 %all-to-all-start.1 = ((f32[16,8,128]{2,1,0:T(8,128)}), f32[16,8,128]{2,1,0:T(8,128)S(1)}, u32[]{:S(2)}, u32[]{:S(2)}) async-start(f32[16,8,128]{2,1,0:T(8,128)} %second.1), calls=%async_computation.1 | async-start | bytes 131072 | tf_op jit(solution)/shard_map/all_to_all | solution.py:370
